TPU v7x, 32 devices: a whole 2x2x4 slice. The times are simulated.
32 devices in a mesh: dp: 8 (over z, x), cent: 4 (over y, core).
Axes of the slice: x: 2, y: 2, z: 4, core: 2. Of those that a mesh axis runs over, the one named last changes fastest.
Arguments:
- documents: bfloat16 [16384, 2048], P(('dp', 'cent')), may hold values from -6 to 6
- assigned: int32 [16384], P(('dp', 'cent')), may hold values from 0 to 12287, as said below
- centroids: bfloat16 [12288, 2048], P(('dp', 'cent')), may hold values from -6 to 6
- owner_slot: int32 [12288], replicated, may hold values from 0 to 12287, as said below
Outputs:
- prototypicality: float32 [16384], P(('dp', 'cent'))
- redundancy: float32 [16384], P(('dp', 'cent'))
- cluster_stats: float32 [3, 12288], P(None, ('dp', 'cent'))
Inputs may be any that keep to these rules, and one draw needn't show every extreme that they name: `owner_slot`: A permutation of the cluster numbers. `assigned`: of the 512 documents of one device, at most 32 have a slot in any one owner's block of 384 slots, and at most 80 have slots with the owners that share one dp index; in every draw some device reaches 80, and one owner receives exactly 32 from every device.
All inputs are finite; a program needn't handle non-finite values.
Results may differ from a plain program's by a relative error of at most 0.0003.
Values may be sent and summed in bfloat16 or wider, within the bound.
No kernel may reach another device: no remote copies, remote signals or barrier semaphores. Data moves between devices by JAX's collectives and lax.ppermute only.
A program may use at most 64 MiB of HBM per device.

v0:
```python
import math

import jax
import jax.numpy as jnp
from jax import lax
from jax.experimental import pallas as pl
from jax.experimental.pallas import tpu as pltpu
from jax.sharding import PartitionSpec as P


LANES = 128
HIGHEST = lax.Precision.HIGHEST


def bucket_positions(target, groups, capacity):
    length = target.shape[0]
    indicator = (target[:, None] == jnp.arange(groups, dtype=jnp.int32)[None, :]).astype(
        jnp.bfloat16
    )
    earlier = (
        lax.broadcasted_iota(jnp.int32, (length, length), 0)
        > lax.broadcasted_iota(jnp.int32, (length, length), 1)
    ).astype(jnp.bfloat16)
    before = jnp.dot(earlier, indicator, preferred_element_type=jnp.float32)
    rank_ids = jnp.sum(before * indicator.astype(jnp.float32), axis=1).astype(jnp.int32)
    return jnp.where(target < groups, target * capacity + rank_ids, groups * capacity)


def owner_work(incoming, incoming_tags, centroids):
    table_rows = centroids.shape[0]
    width = incoming.shape[1]
    length = incoming_tags.shape[0]
    is_live = incoming_tags >= 0
    safe_slot = jnp.clip(incoming_tags, 0, table_rows - 1)
    cent_sq = jnp.einsum("kd,kd->k", centroids, centroids, preferred_element_type=jnp.float32)
    cent_vec = centroids[safe_slot]
    cross_dot = jnp.einsum("sd,sd->s", incoming, cent_vec, preferred_element_type=jnp.float32)
    self_sq = jnp.einsum("sd,sd->s", incoming, incoming, preferred_element_type=jnp.float32)
    inverse_norm = lax.rsqrt(self_sq + 1.0)
    similarity = cross_dot * inverse_norm * lax.rsqrt(cent_sq[safe_slot] + 1.0)
    members = (incoming_tags[:, None] == jnp.arange(table_rows, dtype=jnp.int32)[None, :]).astype(
        jnp.float32
    )
    live_weight = is_live.astype(jnp.float32)
    moments = jnp.stack(
        [live_weight, live_weight * similarity, live_weight * similarity * similarity]
    )
    cluster_totals = jnp.dot(
        moments, members, precision=lax.Precision.HIGHEST, preferred_element_type=jnp.float32
    )
    count_floor = jnp.maximum(cluster_totals[0], 1.0)
    mean_sim = cluster_totals[1] / count_floor
    variance = jnp.maximum(cluster_totals[2] / count_floor - mean_sim * mean_sim, 0.0)
    proto_score = jnp.where(
        is_live,
        (mean_sim[safe_slot] - similarity) / jnp.sqrt(variance[safe_slot] + 1.0 / width),
        0.0,
    )
    gram_block = lax.dot_general(
        incoming, incoming, (((1,), (1,)), ((), ())), preferred_element_type=jnp.float32
    )
    cosine = gram_block * inverse_norm[:, None] * inverse_norm[None, :]
    not_self = lax.broadcasted_iota(jnp.int32, (length, length), 0) != lax.broadcasted_iota(
        jnp.int32, (length, length), 1
    )
    same_cluster = (incoming_tags[:, None] == incoming_tags[None, :]) & is_live[:, None] & not_self
    redundant = math.sqrt(width) * jnp.max(jnp.where(same_cluster, cosine, 0.0), axis=1)
    return (cluster_totals, proto_score, redundant)


def iota(shape, dim):
    return lax.broadcasted_iota(jnp.int32, shape, dim)


def mm(a, b, dims, precision=None):
    return lax.dot_general(
        a, b, (dims, ((), ())), precision=precision, preferred_element_type=jnp.float32
    )


def ring(dp):
    line = dp >> 1
    return line ^ (line >> 1)


def shift(dp, m):
    place = (ring(dp) + (m >> 1)) & 3
    return ((place ^ (place >> 1)) << 1) | ((dp ^ m) & 1)


def back_shift(dp, m):
    return shift(dp, ((8 - (m & 6)) & 6) | (m & 1))


def relative(owner_dp, dp):
    return (((ring(owner_dp) - ring(dp)) & 3) << 1) | ((owner_dp ^ dp) & 1)


def params(mib):
    return pltpu.CompilerParams(vmem_limit_bytes=mib * 1024 * 1024)


def local(documents, assigned, centroids, owner_slot):
    docs, width = documents.shape
    rows = centroids.shape[0]
    dp = lax.axis_size("dp")
    cent = lax.axis_size("cent")
    owners = dp * cent
    cap = 2 * docs // owners
    row_cap = 5 * cent * cap // 8
    group = cent * cap
    clusters = owner_slot.shape[0]
    root = math.sqrt(width)
    far, direct, relayed, stages = plan()
    source = lambda m, e: back_shift(lax.axis_index("dp"), m) * cent + (lax.axis_index("cent") ^ e)
    span = lambda f: (f[1] * width // f[2], (f[1] + 1) * width // f[2])

    def route(assigned_hbm, table_hbm, docs_hbm, far_ref, tag_ref, key_ref, *scratch):
        assigned_ref, table_ref, docs_ref, sems = scratch
        copies = [
            pltpu.make_async_copy(src, dst, sems.at[n])
            for n, (src, dst) in enumerate(
                [(assigned_hbm, assigned_ref), (table_hbm, table_ref), (docs_hbm, docs_ref)]
            )
        ]
        for copy in copies:
            copy.start()
        copies[0].wait()
        copies[1].wait()
        a = assigned_ref[...]
        pick = (iota((clusters // LANES, docs), 0) == a // LANES).astype(jnp.float32)
        lines = mm(table_ref[...].astype(jnp.float32), pick, ((0,), (0,)), HIGHEST)
        slot = jnp.sum(
            jnp.where(iota((LANES, docs), 0) == a % LANES, lines, 0.0), axis=0, keepdims=True
        )
        owner = jnp.floor((slot + 0.5) * (1.0 / rows))
        home = slot - owner * rows + 1.0
        owner = owner.astype(jnp.int32)
        here, side = lax.axis_index("dp"), lax.axis_index("cent")
        rel = relative(owner // cent, here) * cent + ((owner % cent) ^ side)
        which = iota((owners, docs), 0)
        mine = which == owner
        near = which // cent == owner // cent
        earlier = (iota((docs, docs), 0) < iota((docs, docs), 1)).astype(jnp.bfloat16)
        before = mm(mine.astype(jnp.bfloat16), earlier, ((1,), (0,)))
        count = lambda m: jnp.sum(jnp.where(m, before, 0.0), axis=0, keepdims=True)
        rank = count(mine).astype(jnp.int32)
        row_rank = count(near).astype(jnp.int32)
        key = rel * cap + rank
        row_key = (rel // cent) * row_cap + row_rank
        key_ref[0:1, :] = key
        key_ref[1:2, :] = row_key
        key_ref[2:3, :] = owner
        at_rank = (iota((cap, docs), 0) == rank).astype(jnp.float32)
        at_row = (iota((row_cap, docs), 0) == row_rank).astype(jnp.float32)
        homes = mm(jnp.where(mine, home, 0.0), at_rank, ((1,), (1,)), HIGHEST)
        inner = (key % group + 1).astype(jnp.float32)
        inners = mm(jnp.where(near, inner, 0.0), at_row, ((1,), (1,)), HIGHEST)
        tag_ref[...] = jnp.zeros((owners, 1, LANES), jnp.int32)
        tag_ref[:, 0, :cap] = homes.astype(jnp.int32)
        tag_ref[:, 0, cap : cap + row_cap] = inners.astype(jnp.int32)
        sel = iota((row_cap, docs), 0) + far[0][0] * row_cap == row_key
        copies[2].wait()
        picked = mm(sel.astype(jnp.bfloat16), docs_ref[...], ((1,), (0,)))
        far_ref[...] = picked.astype(jnp.bfloat16)

    def pack(key_hbm, docs_hbm, *refs):
        *outs, key_ref, docs_ref, sems = refs
        copies = [
            pltpu.make_async_copy(key_hbm, key_ref, sems.at[0]),
            pltpu.make_async_copy(docs_hbm, docs_ref, sems.at[1]),
        ]
        for copy in copies:
            copy.start()
        copies[0].wait()
        key, row_key = key_ref[0:1, :], key_ref[1:2, :]
        rest = sorted({f[0] for f in far[1:]})
        sel = [iota((row_cap, docs), 0) + m * row_cap == row_key for m in rest]
        sel += [iota((group, docs), 0) + m * group == key for m in direct]
        sel = jnp.concatenate([v.astype(jnp.bfloat16) for v in sel], axis=0)
        copies[1].wait()
        step = width // 4
        for lo in range(0, width, step):
            picked = mm(sel, docs_ref[:, lo : lo + step], ((1,), (0,))).astype(jnp.bfloat16)
            for ref, f in zip(outs, far[1:]):
                at = rest.index(f[0]) * row_cap
                if span(f)[0] <= lo < span(f)[1]:
                    lane = lo - span(f)[0]
                    ref[:, lane : lane + step] = picked[at : at + row_cap]
            for n, ref in enumerate(outs[len(far) - 1 :]):
                at = len(rest) * row_cap + n * cap
                ref[:, lo : lo + step] = picked[at : at + cap]

    def norms(cent_ref, keep_ref, inv_ref):
        keep_ref[...] = cent_ref[...]
        c = cent_ref[...].astype(jnp.float32)
        inv_ref[...] = lax.rsqrt(jnp.sum(c * c, axis=1, keepdims=True) + 1.0)

    def make_relay(part):
        def body(tag_ref, *refs):
            for n, (m, _, _) in enumerate(part):
                tags = tag_ref[pl.ds(source(m, 0), 1), 0, cap : cap + row_cap]
                sel = (iota((group, row_cap), 0) + 1 == tags).astype(jnp.bfloat16)
                picked = mm(sel, refs[n][...], ((1,), (0,))).astype(jnp.bfloat16)
                for e in range(cent):
                    refs[len(part) + e][n * cap : (n + 1) * cap] = picked[e * cap : (e + 1) * cap]

        return body

    def make_owner(s):
        parts = stages[s]
        masks = stage_masks(parts)
        fresh = len(masks) * group
        last = s == len(stages) - 1

        def body(*refs):
            refs = list(refs)
            take = lambda n: [refs.pop(0) for _ in range(n)]
            arrays = [take(cent) for _ in parts]
            tag_ref, cent_ref, cent_inv_ref = take(3)
            olds = [take(3) for _ in range(s)]
            tally = take(1)[0] if s else None
            if last:
                score_ref, stat_ref, x = take(3)
            else:
                x, col, line, tally_out = take(4)
                old_outs = take(s)
            for part, refs_e in zip(parts, arrays):
                for i, f in enumerate(part):
                    lo, hi = span(f)
                    for e in range(cent):
                        at = (masks.index(f[0]) * cent + e) * cap
                        x[at : at + cap, lo:hi] = refs_e[e][i * cap : (i + 1) * cap, :]
            tags = [
                tag_ref[pl.ds(source(m, e), 1), 0, :cap] for m in masks for e in range(cent)
            ]
            tag = jnp.concatenate(tags, axis=1).astype(jnp.float32)
            eye = iota((LANES, LANES), 0) == iota((LANES, LANES), 1)

            def to_row(v):
                pieces = [
                    jnp.sum(jnp.where(eye, v[i : i + LANES], 0.0), axis=0, keepdims=True)
                    for i in range(0, v.shape[0], LANES)
                ]
                return jnp.concatenate(pieces, axis=1) if len(pieces) > 1 else pieces[0]

            def to_col(v):
                pieces = [
                    jnp.sum(jnp.where(eye, v[:, i : i + LANES], 0.0), axis=1, keepdims=True)
                    for i in range(0, v.shape[1], LANES)
                ]
                return jnp.concatenate(pieces, axis=0) if len(pieces) > 1 else pieces[0]

            cent_inv = cent_inv_ref[...]
            if s == 0:
                counts = [jnp.zeros((rows, 1), jnp.float32)] * 3
            else:
                counts = [tally[:, i : i + 1] for i in range(3)]
            xn = x[...]
            own_gram = mm(xn, xn, ((1,), (1,)))
            cols, lines = [], []
            for i in range(0, fresh, LANES):
                diag = jnp.where(eye, own_gram[i : i + LANES, i : i + LANES], 0.0)
                cols.append(lax.rsqrt(jnp.sum(diag, axis=1, keepdims=True) + 1.0))
                lines.append(lax.rsqrt(jnp.sum(diag, axis=0, keepdims=True) + 1.0))
            tag_col = to_col(tag)
            inv_col = jnp.concatenate(cols, axis=0)
            inv = jnp.concatenate(lines, axis=1)
            cross = mm(cent_ref[...], xn, ((1,), (1,)))
            own = (iota((rows, fresh), 0) + 1).astype(jnp.float32) == tag
            sim = jnp.sum(jnp.where(own, cross * cent_inv, 0.0), axis=0, keepdims=True) * inv
            add = lambda v: jnp.sum(jnp.where(own, v, 0.0), axis=1, keepdims=True)
            counts = [c + add(v) for c, v in zip(counts, (jnp.ones_like(sim), sim, sim * sim))]
            same = (tag_col == tag) & (iota((fresh, fresh), 0) != iota((fresh, fresh), 1))
            best = jnp.max(jnp.where(same, own_gram * inv_col, 0.0), axis=0, keepdims=True)
            old_best = []
            for x_old, col_old, line_old in olds:
                gram = mm(x_old[...], xn, ((1,), (1,)))
                same = col_old[:, 0:1] == tag
                up = jnp.max(
                    jnp.where(same, gram * col_old[:, 1:2], 0.0), axis=0, keepdims=True
                )
                best = jnp.maximum(best, up)
                down = jnp.max(jnp.where(same, gram * inv, 0.0), axis=1, keepdims=True)
                old_best.append(jnp.maximum(line_old[3:4, :], to_row(down)))
            if not last:
                col[:, 0:1] = tag_col
                col[:, 1:2] = inv_col
                for i, v in enumerate((tag, inv, sim, best)):
                    line[i : i + 1, :] = v
                for i, v in enumerate(counts):
                    tally_out[:, i : i + 1] = v
                for ref, (_, _, line_old), v in zip(old_outs, olds, old_best):
                    ref[0:3, :] = line_old[0:3, :]
                    ref[3:4, :] = v
                return
            floor = jnp.maximum(counts[0], 1.0)
            mean = counts[1] / floor
            var = jnp.maximum(counts[2] / floor - mean * mean, 0.0)
            spread = 1.0 / jnp.sqrt(var + 1.0 / width)
            for i, v in enumerate(counts):
                stat_ref[i : i + 1, :] = to_row(v)
            facts = [(l[0:1, :], l[1:2, :], l[2:3, :], b) for (_, _, l), b in zip(olds, old_best)]
            facts.append((tag, inv, sim, best))
            for parts_s, (tag, inv, sim, best) in zip(stages, facts):
                order_s = stage_masks(parts_s)
                own = (iota((rows, tag.shape[1]), 0) + 1).astype(jnp.float32) == tag
                pick = lambda v: jnp.sum(jnp.where(own, v, 0.0), axis=0, keepdims=True)
                score = (pick(mean) - sim) * pick(spread)
                red = best * inv * root
                for b in range(len(order_s) * cent):
                    part = slice(b * cap, (b + 1) * cap)
                    score_ref[pl.ds(source(order_s[b // cent], b % cent), 1), 0, :] = jnp.concatenate(
                        [score[:, part], red[:, part]], axis=1
                    )

        return body

    def unpack(score_ref, key_ref, out_ref, red_ref):
        key = key_ref[0:1, :]
        pick = (iota((owners, docs), 0) == key_ref[2:3, :]).astype(jnp.float32)
        got = mm(score_ref[:, 0, :], pick, ((0,), (0,)), HIGHEST)
        rank = iota((2 * cap, docs), 0)
        out_ref[...] = jnp.sum(jnp.where(rank == key % cap, got, 0.0), axis=0, keepdims=True)
        red_ref[...] = jnp.sum(jnp.where(rank == key % cap + cap, got, 0.0), axis=0, keepdims=True)

    f32 = lambda *s: jax.ShapeDtypeStruct(s, jnp.float32)
    bf16 = lambda *s: jax.ShapeDtypeStruct(s, jnp.bfloat16)
    i32 = lambda *s: jax.ShapeDtypeStruct(s, jnp.int32)
    cost = lambda n: pl.CostEstimate(flops=n, bytes_accessed=1 << 20, transcendentals=0)

    def call(body, ins, outs, flops, scratch=(), mib=16, space=pltpu.VMEM):
        return pl.pallas_call(
            body,
            out_shape=outs,
            in_specs=[pl.BlockSpec(memory_space=space)] * len(ins),
            out_specs=[pl.BlockSpec(memory_space=pltpu.VMEM)] * len(outs),
            scratch_shapes=list(scratch),
            compiler_params=params(mib),
            cost_estimate=cost(flops),
        )(*ins)

    def send(value, m, e):
        if not m and not e:
            return value
        if not e:
            return lax.ppermute(value, "dp", [(i, shift(i, m)) for i in range(dp)])
        if not m:
            return lax.ppermute(value, "cent", [(j, j ^ e) for j in range(cent)])
        pairs = [
            (i * cent + j, shift(i, m) * cent + (j ^ e)) for i in range(dp) for j in range(cent)
        ]
        return lax.ppermute(value, ("dp", "cent"), pairs)

    def exchange(value):
        return lax.all_to_all(value, ("dp", "cent"), 0, 0, tiled=True)

    table = owner_slot.reshape(-1, LANES)
    held = pltpu.VMEM((docs, width), jnp.bfloat16)
    first, tags, key = call(
        route,
        (assigned.reshape(1, docs), table, documents),
        [bf16(row_cap, width), i32(owners, 1, LANES), i32(8, docs)],
        2 * row_cap * docs * width,
        [
            pltpu.VMEM((1, docs), jnp.int32),
            pltpu.VMEM(table.shape, jnp.int32),
            held,
            pltpu.SemaphoreType.DMA((3,)),
        ],
        mib=63,
        space=pl.ANY,
    )
    tags = exchange(tags)
    got = call(
        pack,
        (key, documents),
        [bf16(row_cap, width // f[2]) for f in far[1:]]
        + [bf16(cap, width)] * (len(direct) * cent),
        2 * len(far) * row_cap * docs * width,
        [pltpu.VMEM((8, docs), jnp.int32), held, pltpu.SemaphoreType.DMA((2,))],
        mib=63,
        space=pl.ANY,
    )
    sent = {f: send(v, f[0], 0) for f, v in zip(far, [first, *got])}
    arrays = {}
    for n, m in enumerate(direct):
        near = got[len(far) - 1 + n * cent : len(far) - 1 + (n + 1) * cent]
        arrays[((m, 0, 1),)] = [send(v, m, e) for e, v in enumerate(near)]
    for part in relayed:
        size = width // part[0][2]
        hop = call(
            make_relay(part),
            (tags, *[sent[f] for f in part]),
            [bf16(len(part) * cap, size)] * cent,
            2 * len(part) * group * row_cap * size,
        )
        arrays[part] = [send(hop[e], 0, e) for e in range(cent)]
    kept, cent_inv = call(norms, (centroids,), [bf16(rows, width), f32(rows, 1)], 2 * rows * width)
    olds, tally = [], None
    for s, parts in enumerate(stages):
        fresh = len(stage_masks(parts)) * group
        ins = [b for part in parts for b in arrays[part]] + [tags, kept, cent_inv]
        ins += [v for old in olds for v in old] + ([tally] if s else [])
        flops = 2 * fresh * (rows + fresh + sum(o[0].shape[0] for o in olds)) * width
        if s < len(stages) - 1:
            outs = [bf16(fresh, width), f32(fresh, 2), f32(4, fresh), f32(rows, 3)]
            outs += [f32(*o[2].shape) for o in olds]
            x, col, line, tally, *lines = call(make_owner(s), ins, outs, flops)
            olds = [(o[0], o[1], l) for o, l in zip(olds, lines)] + [(x, col, line)]
        else:
            scratch = [pltpu.VMEM((fresh, width), jnp.bfloat16)]
            outs = [f32(owners, 1, 2 * cap), f32(3, rows)]
            scores, stats = call(make_owner(s), ins, outs, flops, scratch)
    back = exchange(scores)
    proto, red = call(unpack, (back, key), [f32(1, docs)] * 2, 1 << 20)
    return proto.reshape(docs), red.reshape(docs), stats


def stage_masks(parts):
    out = []
    for part in parts:
        out += [f[0] for f in part if f[0] not in out]
    return out


def plan():
    whole = lambda *masks: tuple((m, 0, 1) for m in masks)
    lo, hi = (5, 0, 2), (5, 1, 2)
    far = [f[0] for f in map(whole, (4, 2, 6, 3, 7))] + [lo, hi]
    relayed = [(f,) for f in far]
    direct = [0, 1]
    stages = [
        [whole(0), whole(1)],
        [whole(4), whole(2), whole(6)],
        [whole(3), whole(7)],
        [(lo,), (hi,)],
    ]
    return far, direct, relayed, stages


def local_general(documents, assigned, centroids, owner_slot):
    doc_count, width = documents.shape
    table_rows = centroids.shape[0]
    dp_count = lax.axis_size("dp")
    cent_count = lax.axis_size("cent")
    owner_count = dp_count * cent_count
    pair_cap = 2 * doc_count // owner_count
    row_cap = 5 * cent_count * pair_cap // 8
    slot_ids = owner_slot[assigned]
    owner_ids = slot_ids // table_rows
    local_ids = slot_ids % table_rows
    row_ids = owner_ids // cent_count
    col_ids = owner_ids % cent_count
    first_pos = bucket_positions(row_ids, dp_count, row_cap)
    outgoing = jnp.zeros((dp_count * row_cap, width), jnp.bfloat16).at[first_pos].set(documents)
    tag_ids = (
        jnp.full((dp_count * row_cap,), -1, jnp.int32)
        .at[first_pos]
        .set(col_ids * table_rows + local_ids)
    )
    relayed, relayed_tags = (
        lax.all_to_all(
            outgoing.reshape(dp_count, row_cap, width),
            "dp",
            split_axis=0,
            concat_axis=0,
            tiled=True,
        ),
        lax.all_to_all(
            tag_ids.reshape(dp_count, row_cap), "dp", split_axis=0, concat_axis=0, tiled=True
        ),
    )
    relayed = relayed.reshape(-1, width)
    relayed_tags = relayed_tags.reshape(-1)
    relay_live = relayed_tags >= 0
    relay_target = jnp.where(relay_live, relayed_tags // table_rows, cent_count)
    inner_cap = dp_count * pair_cap
    second_pos = bucket_positions(relay_target, cent_count, inner_cap)
    forward = (
        jnp.zeros((cent_count * inner_cap, width), jnp.bfloat16)
        .at[second_pos]
        .set(relayed, mode="drop")
    )
    forward_tags = (
        jnp.full((cent_count * inner_cap,), -1, jnp.int32)
        .at[second_pos]
        .set(jnp.where(relay_live, relayed_tags % table_rows, -1), mode="drop")
    )
    incoming, incoming_tags = (
        lax.all_to_all(
            forward.reshape(cent_count, inner_cap, width),
            "cent",
            split_axis=0,
            concat_axis=0,
            tiled=True,
        ),
        lax.all_to_all(
            forward_tags.reshape(cent_count, inner_cap),
            "cent",
            split_axis=0,
            concat_axis=0,
            tiled=True,
        ),
    )
    cluster_totals, proto_score, redundant = owner_work(
        incoming.reshape(-1, width), incoming_tags.reshape(-1), centroids
    )
    back_score, back_redundant = (
        lax.all_to_all(
            proto_score.reshape(cent_count, inner_cap),
            "cent",
            split_axis=0,
            concat_axis=0,
            tiled=True,
        ),
        lax.all_to_all(
            redundant.reshape(cent_count, inner_cap),
            "cent",
            split_axis=0,
            concat_axis=0,
            tiled=True,
        ),
    )
    safe_pos = jnp.clip(second_pos, 0, cent_count * inner_cap - 1)
    relay_score = jnp.where(relay_live, back_score.reshape(-1)[safe_pos], 0.0)
    relay_redundant = jnp.where(relay_live, back_redundant.reshape(-1)[safe_pos], 0.0)
    home_score, home_redundant = (
        lax.all_to_all(
            relay_score.reshape(dp_count, row_cap), "dp", split_axis=0, concat_axis=0, tiled=True
        ),
        lax.all_to_all(
            relay_redundant.reshape(dp_count, row_cap),
            "dp",
            split_axis=0,
            concat_axis=0,
            tiled=True,
        ),
    )
    prototypicality = home_score.reshape(-1)[first_pos]
    redundancy = home_redundant.reshape(-1)[first_pos]
    return (prototypicality, redundancy, cluster_totals)


def solution(mesh):
    in_specs = (P(("dp", "cent"), None), P(("dp", "cent")), P(("dp", "cent"), None), P())
    out_specs = (P(("dp", "cent")), P(("dp", "cent")), P(None, ("dp", "cent")))
    dp, cent = mesh.shape["dp"], mesh.shape["cent"]
    small = dp == 8 and cent & (cent - 1) == 0

    def body(*args):
        return (local if small else local_general)(*args)

    return jax.shard_map(body, mesh=mesh, in_specs=in_specs, out_specs=out_specs, check_vma=False)
```

profile of v0, /device:TPU:0, one launch (start us, length us, event | category | flops | bytes accessed | tf_op | source)
XLA Modules:
  0.0 131.5 jit_solution(14530247280095601580)
XLA Ops:
  0.6 3.2 %shard_map.67 = (bf16[80,2048]{1,0:T(8,128)(2,1)}, s32[32,1,128]{2,1,0:T(1,128)}, s32[8,512]{1,0:T(8,128)}) custom-call(s32[1,512]{1,0:T(1,128)} %bitcast.5, s32[96,128]{1,0:T(8,128)} %bitcast.4, bf16[512,2048]{1,0:T(8,128)(2,1)} %docs_hbm.3), custom_call_target="tpu_custom_call" | custom-call | flops 167772160 | bytes 1048576 | tf_op jit(solution)/shard_map/pallas_call | solution.py:333
  3.9 4.6 %shard_map.68 = (bf16[80,2048]{1,0:T(8,128)(2,1)}, bf16[80,2048]{1,0:T(8,128)(2,1)}, bf16[80,2048]{1,0:T(8,128)(2,1)}, bf16[80,2048]{1,0:T(8,128)(2,1)}, bf16[80...) custom-call(s32[8,512]{1,0:T(8,128)} %get-tuple-element.70.key_hbm.k, ...), custom_call_target="tpu_custom_call" | custom-call | flops 1174405120 | bytes 1048576 | tf_op jit(solution)/shard_map/pallas_call | solution.py:333
  8.5 2.5 %collective-permute-start.10 = (bf16[32,2048]{1,0:T(8,128)(2,1)}, bf16[32,2048]{1,0:T(8,128)(2,1)S(1)}, u32[]{:S(2)}, u32[]{:S(2)}) collective-permute-start(bf16[32,2048]{1,0:T(8,128)(2,1)} %get-tuple-element.86), channel_id=1, source_target_pairs={{0,3},{1,2},{2,1},{3,0},{4,7},{5,6},{6,5},{7,4},{8,11},{9,10},{10,... | collective-permute-start | bytes 393224 | tf_op jit(solution)/shard_map/ppermute | solution.py:349
  11.0 1.5 %collective-permute-start.11 = (bf16[32,2048]{1,0:T(8,128)(2,1)}, bf16[32,2048]{1,0:T(8,128)(2,1)S(1)}, u32[]{:S(2)}, u32[]{:S(2)}) collective-permute-start(bf16[32,2048]{1,0:T(8,128)(2,1)} %get-tuple-element.87), channel_id=1, source_target_pairs={{0,4},{4,0},{8,12},{12,8},{16,20},{20,16},{24,28},{28,24},{1,5},{5... | collective-permute-start | bytes 393224 | tf_op jit(solution)/shard_map/ppermute | solution.py:347
  12.5 0.5 collective-permute-start.12
  13.0 1.4 %collective-permute-start.13 = (bf16[32,2048]{1,0:T(8,128)(2,1)}, bf16[32,2048]{1,0:T(8,128)(2,1)S(1)}, u32[]{:S(2)}, u32[]{:S(2)}) collective-permute-start(bf16[32,2048]{1,0:T(8,128)(2,1)} %get-tuple-element.89), channel_id=1, source_target_pairs={{0,6},{1,7},{2,4},{3,5},{4,2},{5,3},{6,0},{7,1},{8,14},{9,15},{10,... | collective-permute-start | bytes 393224 | tf_op jit(solution)/shard_map/ppermute | solution.py:353
  14.4 0.9 collective-permute-start.14
  15.4 2.2 %collective-permute-start.27 = (bf16[80,2048]{1,0:T(8,128)(2,1)}, bf16[80,2048]{1,0:T(8,128)(2,1)S(1)}, u32[]{:S(2)}, u32[]{:S(2)}) collective-permute-start(bf16[80,2048]{1,0:T(8,128)(2,1)} %get-tuple-element.108), channel_id=1, source_target_pairs={{0,8},{4,12},{8,24},{12,28},{16,0},{20,4},{24,16},{28,20},{1,9},{5... | collective-permute-start | bytes 983048 | tf_op jit(solution)/shard_map/ppermute | solution.py:347
  17.5 4.5 %collective-permute-start.4 = (bf16[80,1024]{1,0:T(8,128)(2,1)}, bf16[80,1024]{1,0:T(8,128)(2,1)S(1)}, u32[]{:S(2)}, u32[]{:S(2)}) collective-permute-start(bf16[80,1024]{1,0:T(8,128)(2,1)} %get-tuple-element.76), channel_id=1, source_target_pairs={{0,28},{4,24},{8,20},{12,16},{16,12},{20,8},{24,4},{28,0},{1,29},{... | collective-permute-start | bytes 491528 | tf_op jit(solution)/shard_map/ppermute | solution.py:347
  22.1 1.2 collective-permute-done.13.refs_6_
  23.2 1.4 %collective-permute-start.9 = (bf16[32,2048]{1,0:T(8,128)(2,1)}, bf16[32,2048]{1,0:T(8,128)(2,1)S(1)}, u32[]{:S(2)}, u32[]{:S(2)}) collective-permute-start(bf16[32,2048]{1,0:T(8,128)(2,1)} %get-tuple-element.85), channel_id=1, source_target_pairs={{0,2},{1,3},{2,0},{3,1},{4,6},{5,7},{6,4},{7,5},{8,10},{9,11},{10,... | collective-permute-start | bytes 393224 | tf_op jit(solution)/shard_map/ppermute | solution.py:349
  24.8 3.0 %collective-permute-start.31 = (bf16[80,2048]{1,0:T(8,128)(2,1)}, bf16[80,2048]{1,0:T(8,128)(2,1)S(1)}, u32[]{:S(2)}, u32[]{:S(2)}) collective-permute-start(bf16[80,2048]{1,0:T(8,128)(2,1)} %get-tuple-element.113), channel_id=1, source_target_pairs={{0,16},{4,20},{8,0},{12,4},{16,24},{20,28},{24,8},{28,12},{1,17},{... | collective-permute-start | bytes 983048 | tf_op jit(solution)/shard_map/ppermute | solution.py:347
  27.8 1.3 %collective-permute-start.23 = (bf16[80,2048]{1,0:T(8,128)(2,1)S(1)}, bf16[80,2048]{1,0:T(8,128)(2,1)S(1)}, u32[]{:S(2)}, u32[]{:S(2)}) collective-permute-start(bf16[80,2048]{1,0:T(8,128)(2,1)S(1)} %copy-done.4), channel_id=1, source_target_pairs={{0,24},{4,28},{8,16},{12,20},{16,8},{20,12},{24,0},{28,4},{1,25},{... | collective-permute-start | bytes 983048 | tf_op jit(solution)/shard_map/ppermute | solution.py:347
  29.1 1.8 %collective-permute-start.15 = (bf16[80,2048]{1,0:T(8,128)(2,1)}, bf16[80,2048]{1,0:T(8,128)(2,1)S(1)}, u32[]{:S(2)}, u32[]{:S(2)}) collective-permute-start(bf16[80,2048]{1,0:T(8,128)(2,1)} %get-tuple-element.93), channel_id=1, source_target_pairs={{0,12},{4,8},{8,28},{12,24},{16,4},{20,0},{24,20},{28,16},{1,13},{... | collective-permute-start | bytes 983048 | tf_op jit(solution)/shard_map/ppermute | solution.py:347
  30.9 2.4 %collective-permute-done.4.refs_0_ = bf16[80,1024]{1,0:T(8,128)(2,1)S(1)} collective-permute-done((bf16[80,1024]{1,0:T(8,128)(2,1)}, bf16[80,1024]{1,0:T(8,128)(2,1)S(1)}, u32[]{:S(2)}, u32[]{:S(2)}) %collective-permute-start.4) | collective-permute-done | bytes 163872 | tf_op jit(solution)/shard_map/ppermute | solution.py:347
  33.3 21.4 %collective-permute-start.19 = (bf16[80,2048]{1,0:T(8,128)(2,1)}, bf16[80,2048]{1,0:T(8,128)(2,1)S(1)}, u32[]{:S(2)}, u32[]{:S(2)}) collective-permute-start(bf16[80,2048]{1,0:T(8,128)(2,1)} %get-tuple-element.98), channel_id=1, source_target_pairs={{0,20},{4,16},{8,4},{12,0},{16,28},{20,24},{24,12},{28,8},{1,21},{... | collective-permute-start | bytes 983048 | tf_op jit(solution)/shard_map/ppermute | solution.py:347
  54.7 24.0 %all_to_all.10.tag_ref.refs_8_.refs_12_ = s32[32,1,128]{2,1,0:T(1,128)S(1)} all-to-all(s32[32,1,128]{2,1,0:T(1,128)S(1)} %copy-done.3), channel_id=1, replica_groups=mesh['dp'=8,'cent'=4] {'dp','cent'}, dimensions={0} | all-to-all | bytes 32768 | tf_op jit(solution)/shard_map/all_to_all | solution.py:356
  79.8 0.6 collective-permute-start.28
  80.3 0.5 collective-permute-start.29
  80.9 0.9 collective-permute-start.30
  81.8 0.7 collective-permute-start.32
  82.5 0.5 collective-permute-start.33
  83.7 0.9 collective-permute-start.34
  84.7 2.0 %collective-permute-done.29.refs_6_ = bf16[32,2048]{1,0:T(8,128)(2,1)S(1)} collective-permute-done((bf16[32,2048]{1,0:T(8,128)(2,1)S(1)}, bf16[32,2048]{1,0:T(8,128)(2,1)S(1)}, u32[]{:S(2)}, u32[]{:S(2)}) %collective-permute-start.29) | collective-permute-done | bytes 131104 | tf_op jit(solution)/shard_map/ppermute | solution.py:349
  86.7 1.1 collective-permute-done.30.refs_7_
  87.8 1.2 collective-permute-start.25
  89.1 1.6 %collective-permute-start.26 = (bf16[32,2048]{1,0:T(8,128)(2,1)S(1)}, bf16[32,2048]{1,0:T(8,128)(2,1)S(1)}, u32[]{:S(2)}, u32[]{:S(2)}) collective-permute-start(bf16[32,2048]{1,0:T(8,128)(2,1)S(1)} %get-tuple-element.107), channel_id=1, source_target_pairs={{0,3},{1,2},{2,1},{3,0},{4,7},{5,6},{6,5},{7,4},{8,11},{9,10},{10,... | collective-permute-start | bytes 393224 | tf_op jit(solution)/shard_map/ppermute | solution.py:349
  90.7 1.6 %collective-permute-done.33.refs_10_ = bf16[32,2048]{1,0:T(8,128)(2,1)S(1)} collective-permute-done((bf16[32,2048]{1,0:T(8,128)(2,1)S(1)}, bf16[32,2048]{1,0:T(8,128)(2,1)S(1)}, u32[]{:S(2)}, u32[]{:S(2)}) %collective-permute-start.33) | collective-permute-done | bytes 131104 | tf_op jit(solution)/shard_map/ppermute | solution.py:349
  92.3 0.4 shard_map.71
  92.7 1.2 shard_map.72
  94.6 0.6 collective-permute-start.17
  95.3 1.3 %collective-permute-start.18 = (bf16[32,2048]{1,0:T(8,128)(2,1)S(1)}, bf16[32,2048]{1,0:T(8,128)(2,1)S(1)}, u32[]{:S(2)}, u32[]{:S(2)}) collective-permute-start(bf16[32,2048]{1,0:T(8,128)(2,1)S(1)} %get-tuple-element.97), channel_id=1, source_target_pairs={{0,3},{1,2},{2,1},{3,0},{4,7},{5,6},{6,5},{7,4},{8,11},{9,10},{10,... | collective-permute-start | bytes 393224 | tf_op jit(solution)/shard_map/ppermute | solution.py:349
  96.6 1.3 %collective-permute-done.25.refs_2_ = bf16[32,2048]{1,0:T(8,128)(2,1)S(1)} collective-permute-done((bf16[32,2048]{1,0:T(8,128)(2,1)S(1)}, bf16[32,2048]{1,0:T(8,128)(2,1)S(1)}, u32[]{:S(2)}, u32[]{:S(2)}) %collective-permute-start.25) | collective-permute-done | bytes 131104 | tf_op jit(solution)/shard_map/ppermute | solution.py:349
  97.9 1.1 collective-permute-done.26.refs_3_
  99.0 1.2 collective-permute-start.21
  100.3 1.6 %collective-permute-start.22 = (bf16[32,2048]{1,0:T(8,128)(2,1)S(1)}, bf16[32,2048]{1,0:T(8,128)(2,1)S(1)}, u32[]{:S(2)}, u32[]{:S(2)}) collective-permute-start(bf16[32,2048]{1,0:T(8,128)(2,1)S(1)} %get-tuple-element.102), channel_id=1, source_target_pairs={{0,3},{1,2},{2,1},{3,0},{4,7},{5,6},{6,5},{7,4},{8,11},{9,10},{10,... | collective-permute-start | bytes 393224 | tf_op jit(solution)/shard_map/ppermute | solution.py:349
  101.9 2.6 %shard_map.78 = (bf16[384,2048]{1,0:T(8,128)(2,1)S(1)}, f32[384,2]{1,0:T(8,128)S(1)}, f32[4,384]{1,0:T(4,128)S(1)}, f32[384,3]{1,0:T(8,128)S(1)}, f32[4,256]{1,0:T(4,128)S(1)}) custom-call(bf16[32,2048]{1,0:T(8,128)(2,1)S(1)} %get-tuple-element.104.refs_0_, bf16[32,2048]{1,0:T(8,128)(2,1)S(1)} %collective-permute-done.24.refs_1_, ...), custom_call_target="tpu_custom_call" | custom-call | flops 1610612736 | bytes 1048576 | tf_op jit(solution)/shard_map/pallas_call | solution.py:333
  104.5 0.6 collective-permute-start.6
  105.1 1.2 collective-permute-start.7
  106.7 2.4 %collective-permute-done.21.refs_6_ = bf16[32,2048]{1,0:T(8,128)(2,1)S(1)} collective-permute-done((bf16[32,2048]{1,0:T(8,128)(2,1)S(1)}, bf16[32,2048]{1,0:T(8,128)(2,1)S(1)}, u32[]{:S(2)}, u32[]{:S(2)}) %collective-permute-start.21) | collective-permute-done | bytes 131104 | tf_op jit(solution)/shard_map/ppermute | solution.py:349
  109.2 0.5 collective-permute-start.2
  109.7 0.6 collective-permute-done.22.refs_7_
  110.3 2.0 %collective-permute-start.3 = (bf16[32,1024]{1,0:T(8,128)(2,1)S(1)}, bf16[32,1024]{1,0:T(8,128)(2,1)S(1)}, u32[]{:S(2)}, u32[]{:S(2)}) collective-permute-start(bf16[32,1024]{1,0:T(8,128)(2,1)S(1)} %get-tuple-element.75), channel_id=1, source_target_pairs={{0,3},{1,2},{2,1},{3,0},{4,7},{5,6},{6,5},{7,4},{8,11},{9,10},{10,... | collective-permute-start | bytes 196616 | tf_op jit(solution)/shard_map/ppermute | solution.py:349
  112.2 1.9 %shard_map.79 = (bf16[256,2048]{1,0:T(8,128)(2,1)S(1)}, f32[256,2]{1,0:T(8,128)S(1)}, f32[4,256]{1,0:T(4,128)S(1)}, f32[384,3]{1,0:T(8,128)S(1)}, f32[4,256]{1,0:T(4,128)S(1)}, /*index=5*/f32[4,384]{1,0:T(4,128)S(1)}) custom-call(bf16[32,2048]{1,0:T(8,128)(2,1)S(1)} %get-tuple-element.94.refs_0_, bf16[32,2048]{1,0:T(8,128)(2,1)S(1)} %collective-permute-done.16.refs_1_, ...), custom_call_target="tpu_custom_call" | custom-call | flops 1342177280 | bytes 1048576 | tf_op jit(solution)/shard_map/pallas_call | solution.py:333
  114.2 1.9 %collective-permute-done.2.refs_2_ = bf16[32,1024]{1,0:T(8,128)(2,1)S(1)} collective-permute-done((bf16[32,1024]{1,0:T(8,128)(2,1)S(1)}, bf16[32,1024]{1,0:T(8,128)(2,1)S(1)}, u32[]{:S(2)}, u32[]{:S(2)}) %collective-permute-start.2) | collective-permute-done | bytes 65568 | tf_op jit(solution)/shard_map/ppermute | solution.py:349
  116.1 2.4 %shard_map.80 = (f32[32,1,64]{2,1,0:T(1,128)S(1)}, f32[3,384]{1,0:T(4,128)}) custom-call(bf16[32,1024]{1,0:T(8,128)(2,1)S(1)} %get-tuple-element.72.refs_0_, bf16[32,1024]{1,0:T(8,128)(2,1)S(1)} %collective-permute-done.1.refs_1_, bf16[32,1024]{1,0:T(8,128)(2,1)S(1)} %collective-permute-done.2.refs_2_, bf16[32,1024]{1,0:T(8,128)(2,1)S(1)} %collective-permute-done.3.refs_3_, ...), custom_call_target="tpu_custom_call" | custom-call | flops 738197504 | bytes 1048576 | tf_op jit(solution)/shard_map/pallas_call | solution.py:333
  118.5 12.1 %all_to_all.11.score_ref = f32[32,1,64]{2,1,0:T(1,128)S(1)} all-to-all(f32[32,1,64]{2,1,0:T(1,128)S(1)} %get-tuple-element.131), channel_id=1, replica_groups=mesh['dp'=8,'cent'=4] {'dp','cent'}, dimensions={0} | all-to-all | bytes 16384 | tf_op jit(solution)/shard_map/all_to_all | solution.py:356
  130.6 0.9 shard_map.81
  (49 shorter events, 3.1 us)
Async XLA Ops:
  3.8 24.0 %copy-start.4 = (bf16[80,2048]{1,0:T(8,128)(2,1)S(1)}, bf16[80,2048]{1,0:T(8,128)(2,1)}, u32[]{:S(2)}) copy-start(bf16[80,2048]{1,0:T(8,128)(2,1)} %get-tuple-element.103) | copy-start | bytes 983044
  3.9 50.9 %copy-start.3 = (s32[32,1,128]{2,1,0:T(1,128)S(1)}, s32[32,1,128]{2,1,0:T(1,128)}, u32[]{:S(2)}) copy-start(s32[32,1,128]{2,1,0:T(1,128)} %get-tuple-element.69) | copy-start | bytes 49156
  8.5 83.9 %copy-start = (bf16[384,2048]{1,0:T(8,128)(2,1)S(1)}, bf16[384,2048]{1,0:T(8,128)(2,1)}, u32[]{:S(2)}) copy-start(bf16[384,2048]{1,0:T(8,128)(2,1)} %cent_ref.1) | copy-start | bytes 4718596
  8.5 6.9 %collective-permute-start.10 = (bf16[32,2048]{1,0:T(8,128)(2,1)}, bf16[32,2048]{1,0:T(8,128)(2,1)S(1)}, u32[]{:S(2)}, u32[]{:S(2)}) collective-permute-start(bf16[32,2048]{1,0:T(8,128)(2,1)} %get-tuple-element.86), channel_id=1, source_target_pairs={{0,3},{1,2},{2,1},{3,0},{4,7},{5,6},{6,5},{7,4},{8,11},{9,10},{10,... | collective-permute-start | bytes 393224 | tf_op jit(solution)/shard_map/ppermute | solution.py:349
  11.0 6.6 %collective-permute-start.11 = (bf16[32,2048]{1,0:T(8,128)(2,1)}, bf16[32,2048]{1,0:T(8,128)(2,1)S(1)}, u32[]{:S(2)}, u32[]{:S(2)}) collective-permute-start(bf16[32,2048]{1,0:T(8,128)(2,1)} %get-tuple-element.87), channel_id=1, source_target_pairs={{0,4},{4,0},{8,12},{12,8},{16,20},{20,16},{24,28},{28,24},{1,5},{5... | collective-permute-start | bytes 393224 | tf_op jit(solution)/shard_map/ppermute | solution.py:347
  12.5 9.6 %collective-permute-start.12 = (bf16[32,2048]{1,0:T(8,128)(2,1)}, bf16[32,2048]{1,0:T(8,128)(2,1)S(1)}, u32[]{:S(2)}, u32[]{:S(2)}) collective-permute-start(bf16[32,2048]{1,0:T(8,128)(2,1)} %get-tuple-element.88), channel_id=1, source_target_pairs={{0,5},{1,4},{2,7},{3,6},{4,1},{5,0},{6,3},{7,2},{8,13},{9,12},{10,... | collective-permute-start | bytes 393224 | tf_op jit(solution)/shard_map/ppermute | solution.py:353
  13.0 10.2 %collective-permute-start.13 = (bf16[32,2048]{1,0:T(8,128)(2,1)}, bf16[32,2048]{1,0:T(8,128)(2,1)S(1)}, u32[]{:S(2)}, u32[]{:S(2)}) collective-permute-start(bf16[32,2048]{1,0:T(8,128)(2,1)} %get-tuple-element.89), channel_id=1, source_target_pairs={{0,6},{1,7},{2,4},{3,5},{4,2},{5,3},{6,0},{7,1},{8,14},{9,15},{10,... | collective-permute-start | bytes 393224 | tf_op jit(solution)/shard_map/ppermute | solution.py:353
  14.4 10.4 %collective-permute-start.14 = (bf16[32,2048]{1,0:T(8,128)(2,1)}, bf16[32,2048]{1,0:T(8,128)(2,1)S(1)}, u32[]{:S(2)}, u32[]{:S(2)}) collective-permute-start(bf16[32,2048]{1,0:T(8,128)(2,1)} %get-tuple-element.90), channel_id=1, source_target_pairs={{0,7},{1,6},{2,5},{3,4},{4,3},{5,2},{6,1},{7,0},{8,15},{9,14},{10,... | collective-permute-start | bytes 393224 | tf_op jit(solution)/shard_map/ppermute | solution.py:353
  15.4 39.3 %collective-permute-start.27 = (bf16[80,2048]{1,0:T(8,128)(2,1)}, bf16[80,2048]{1,0:T(8,128)(2,1)S(1)}, u32[]{:S(2)}, u32[]{:S(2)}) collective-permute-start(bf16[80,2048]{1,0:T(8,128)(2,1)} %get-tuple-element.108), channel_id=1, source_target_pairs={{0,8},{4,12},{8,24},{12,28},{16,0},{20,4},{24,16},{28,20},{1,9},{5... | collective-permute-start | bytes 983048 | tf_op jit(solution)/shard_map/ppermute | solution.py:347
  17.5 15.7 %collective-permute-start.4 = (bf16[80,1024]{1,0:T(8,128)(2,1)}, bf16[80,1024]{1,0:T(8,128)(2,1)S(1)}, u32[]{:S(2)}, u32[]{:S(2)}) collective-permute-start(bf16[80,1024]{1,0:T(8,128)(2,1)} %get-tuple-element.76), channel_id=1, source_target_pairs={{0,28},{4,24},{8,20},{12,16},{16,12},{20,8},{24,4},{28,0},{1,29},{... | collective-permute-start | bytes 491528 | tf_op jit(solution)/shard_map/ppermute | solution.py:347
  22.1 5.7 %collective-permute-start.8 = (bf16[32,2048]{1,0:T(8,128)(2,1)}, bf16[32,2048]{1,0:T(8,128)(2,1)S(1)}, u32[]{:S(2)}, u32[]{:S(2)}) collective-permute-start(bf16[32,2048]{1,0:T(8,128)(2,1)} %get-tuple-element.84), channel_id=1, source_target_pairs={{0,1},{1,0},{2,3},{3,2},{4,5},{5,4},{6,7},{7,6},{8,9},{9,8},{10,11... | collective-permute-start | bytes 393224 | tf_op jit(solution)/shard_map/ppermute | solution.py:349
  23.2 5.9 %collective-permute-start.9 = (bf16[32,2048]{1,0:T(8,128)(2,1)}, bf16[32,2048]{1,0:T(8,128)(2,1)S(1)}, u32[]{:S(2)}, u32[]{:S(2)}) collective-permute-start(bf16[32,2048]{1,0:T(8,128)(2,1)} %get-tuple-element.85), channel_id=1, source_target_pairs={{0,2},{1,3},{2,0},{3,1},{4,6},{5,7},{6,4},{7,5},{8,10},{9,11},{10,... | collective-permute-start | bytes 393224 | tf_op jit(solution)/shard_map/ppermute | solution.py:349
  24.8 54.2 %collective-permute-start.31 = (bf16[80,2048]{1,0:T(8,128)(2,1)}, bf16[80,2048]{1,0:T(8,128)(2,1)S(1)}, u32[]{:S(2)}, u32[]{:S(2)}) collective-permute-start(bf16[80,2048]{1,0:T(8,128)(2,1)} %get-tuple-element.113), channel_id=1, source_target_pairs={{0,16},{4,20},{8,0},{12,4},{16,24},{20,28},{24,8},{28,12},{1,17},{... | collective-permute-start | bytes 983048 | tf_op jit(solution)/shard_map/ppermute | solution.py:347
  27.8 53.1 %collective-permute-start.23 = (bf16[80,2048]{1,0:T(8,128)(2,1)S(1)}, bf16[80,2048]{1,0:T(8,128)(2,1)S(1)}, u32[]{:S(2)}, u32[]{:S(2)}) collective-permute-start(bf16[80,2048]{1,0:T(8,128)(2,1)S(1)} %copy-done.4), channel_id=1, source_target_pairs={{0,24},{4,28},{8,16},{12,20},{16,8},{20,12},{24,0},{28,4},{1,25},{... | collective-permute-start | bytes 983048 | tf_op jit(solution)/shard_map/ppermute | solution.py:347
  29.1 52.7 %collective-permute-start.15 = (bf16[80,2048]{1,0:T(8,128)(2,1)}, bf16[80,2048]{1,0:T(8,128)(2,1)S(1)}, u32[]{:S(2)}, u32[]{:S(2)}) collective-permute-start(bf16[80,2048]{1,0:T(8,128)(2,1)} %get-tuple-element.93), channel_id=1, source_target_pairs={{0,12},{4,8},{8,28},{12,24},{16,4},{20,0},{24,20},{28,16},{1,13},{... | collective-permute-start | bytes 983048 | tf_op jit(solution)/shard_map/ppermute | solution.py:347
  33.3 49.2 %collective-permute-start.19 = (bf16[80,2048]{1,0:T(8,128)(2,1)}, bf16[80,2048]{1,0:T(8,128)(2,1)S(1)}, u32[]{:S(2)}, u32[]{:S(2)}) collective-permute-start(bf16[80,2048]{1,0:T(8,128)(2,1)} %get-tuple-element.98), channel_id=1, source_target_pairs={{0,20},{4,16},{8,4},{12,0},{16,28},{20,24},{24,12},{28,8},{1,21},{... | collective-permute-start | bytes 983048 | tf_op jit(solution)/shard_map/ppermute | solution.py:347
  54.7 25.1 %collective-permute-start = (bf16[80,1024]{1,0:T(8,128)(2,1)}, bf16[80,1024]{1,0:T(8,128)(2,1)S(1)}, u32[]{:S(2)}, u32[]{:S(2)}) collective-permute-start(bf16[80,1024]{1,0:T(8,128)(2,1)} %get-tuple-element.71), channel_id=1, source_target_pairs={{0,28},{4,24},{8,20},{12,16},{16,12},{20,8},{24,4},{28,0},{1,29},{... | collective-permute-start | bytes 491528 | tf_op jit(solution)/shard_map/ppermute | solution.py:347
  78.7 14.1 %copy-start.1 = (bf16[32,2048]{1,0:T(8,128)(2,1)S(1)}, bf16[32,2048]{1,0:T(8,128)(2,1)}, u32[]{:S(2)}) copy-start(bf16[32,2048]{1,0:T(8,128)(2,1)} %get-tuple-element.83.refs_0_) | copy-start | bytes 393220
  79.0 1.4 %collective-permute-start.5 = (bf16[32,1024]{1,0:T(8,128)(2,1)S(1)}, bf16[32,1024]{1,0:T(8,128)(2,1)S(1)}, u32[]{:S(2)}, u32[]{:S(2)}) collective-permute-start(bf16[32,1024]{1,0:T(8,128)(2,1)S(1)} %get-tuple-element.78), channel_id=1, source_target_pairs={{0,1},{1,0},{2,3},{3,2},{4,5},{5,4},{6,7},{7,6},{8,9},{9,8},{10,11... | collective-permute-start | bytes 196616 | tf_op jit(solution)/shard_map/ppermute | solution.py:349
  79.8 4.0 %collective-permute-start.28 = (bf16[32,2048]{1,0:T(8,128)(2,1)S(1)}, bf16[32,2048]{1,0:T(8,128)(2,1)S(1)}, u32[]{:S(2)}, u32[]{:S(2)}) collective-permute-start(bf16[32,2048]{1,0:T(8,128)(2,1)S(1)} %get-tuple-element.110), channel_id=1, source_target_pairs={{0,1},{1,0},{2,3},{3,2},{4,5},{5,4},{6,7},{7,6},{8,9},{9,8},{10,11... | collective-permute-start | bytes 393224 | tf_op jit(solution)/shard_map/ppermute | solution.py:349
  80.3 6.4 %collective-permute-start.29 = (bf16[32,2048]{1,0:T(8,128)(2,1)S(1)}, bf16[32,2048]{1,0:T(8,128)(2,1)S(1)}, u32[]{:S(2)}, u32[]{:S(2)}) collective-permute-start(bf16[32,2048]{1,0:T(8,128)(2,1)S(1)} %get-tuple-element.111), channel_id=1, source_target_pairs={{0,2},{1,3},{2,0},{3,1},{4,6},{5,7},{6,4},{7,5},{8,10},{9,11},{10,... | collective-permute-start | bytes 393224 | tf_op jit(solution)/shard_map/ppermute | solution.py:349
  80.9 6.9 %collective-permute-start.30 = (bf16[32,2048]{1,0:T(8,128)(2,1)S(1)}, bf16[32,2048]{1,0:T(8,128)(2,1)S(1)}, u32[]{:S(2)}, u32[]{:S(2)}) collective-permute-start(bf16[32,2048]{1,0:T(8,128)(2,1)S(1)} %get-tuple-element.112), channel_id=1, source_target_pairs={{0,3},{1,2},{2,1},{3,0},{4,7},{5,6},{6,5},{7,4},{8,11},{9,10},{10,... | collective-permute-start | bytes 393224 | tf_op jit(solution)/shard_map/ppermute | solution.py:349
  81.8 7.2 %collective-permute-start.32 = (bf16[32,2048]{1,0:T(8,128)(2,1)S(1)}, bf16[32,2048]{1,0:T(8,128)(2,1)S(1)}, u32[]{:S(2)}, u32[]{:S(2)}) collective-permute-start(bf16[32,2048]{1,0:T(8,128)(2,1)S(1)} %get-tuple-element.115), channel_id=1, source_target_pairs={{0,1},{1,0},{2,3},{3,2},{4,5},{5,4},{6,7},{7,6},{8,9},{9,8},{10,11... | collective-permute-start | bytes 393224 | tf_op jit(solution)/shard_map/ppermute | solution.py:349
  82.5 9.8 %collective-permute-start.33 = (bf16[32,2048]{1,0:T(8,128)(2,1)S(1)}, bf16[32,2048]{1,0:T(8,128)(2,1)S(1)}, u32[]{:S(2)}, u32[]{:S(2)}) collective-permute-start(bf16[32,2048]{1,0:T(8,128)(2,1)S(1)} %get-tuple-element.116), channel_id=1, source_target_pairs={{0,2},{1,3},{2,0},{3,1},{4,6},{5,7},{6,4},{7,5},{8,10},{9,11},{10,... | collective-permute-start | bytes 393224 | tf_op jit(solution)/shard_map/ppermute | solution.py:349
  83.7 10.9 %collective-permute-start.34 = (bf16[32,2048]{1,0:T(8,128)(2,1)S(1)}, bf16[32,2048]{1,0:T(8,128)(2,1)S(1)}, u32[]{:S(2)}, u32[]{:S(2)}) collective-permute-start(bf16[32,2048]{1,0:T(8,128)(2,1)S(1)} %get-tuple-element.117), channel_id=1, source_target_pairs={{0,3},{1,2},{2,1},{3,0},{4,7},{5,6},{6,5},{7,4},{8,11},{9,10},{10,... | collective-permute-start | bytes 393224 | tf_op jit(solution)/shard_map/ppermute | solution.py:349
  86.7 8.6 %collective-permute-start.24 = (bf16[32,2048]{1,0:T(8,128)(2,1)S(1)}, bf16[32,2048]{1,0:T(8,128)(2,1)S(1)}, u32[]{:S(2)}, u32[]{:S(2)}) collective-permute-start(bf16[32,2048]{1,0:T(8,128)(2,1)S(1)} %get-tuple-element.105), channel_id=1, source_target_pairs={{0,1},{1,0},{2,3},{3,2},{4,5},{5,4},{6,7},{7,6},{8,9},{9,8},{10,11... | collective-permute-start | bytes 393224 | tf_op jit(solution)/shard_map/ppermute | solution.py:349
  87.8 10.1 %collective-permute-start.25 = (bf16[32,2048]{1,0:T(8,128)(2,1)S(1)}, bf16[32,2048]{1,0:T(8,128)(2,1)S(1)}, u32[]{:S(2)}, u32[]{:S(2)}) collective-permute-start(bf16[32,2048]{1,0:T(8,128)(2,1)S(1)} %get-tuple-element.106), channel_id=1, source_target_pairs={{0,2},{1,3},{2,0},{3,1},{4,6},{5,7},{6,4},{7,5},{8,10},{9,11},{10,... | collective-permute-start | bytes 393224 | tf_op jit(solution)/shard_map/ppermute | solution.py:349
  89.1 10.0 %collective-permute-start.26 = (bf16[32,2048]{1,0:T(8,128)(2,1)S(1)}, bf16[32,2048]{1,0:T(8,128)(2,1)S(1)}, u32[]{:S(2)}, u32[]{:S(2)}) collective-permute-start(bf16[32,2048]{1,0:T(8,128)(2,1)S(1)} %get-tuple-element.107), channel_id=1, source_target_pairs={{0,3},{1,2},{2,1},{3,0},{4,7},{5,6},{6,5},{7,4},{8,11},{9,10},{10,... | collective-permute-start | bytes 393224 | tf_op jit(solution)/shard_map/ppermute | solution.py:349
  92.3 8.0 %collective-permute-start.16 = (bf16[32,2048]{1,0:T(8,128)(2,1)S(1)}, bf16[32,2048]{1,0:T(8,128)(2,1)S(1)}, u32[]{:S(2)}, u32[]{:S(2)}) collective-permute-start(bf16[32,2048]{1,0:T(8,128)(2,1)S(1)} %get-tuple-element.95), channel_id=1, source_target_pairs={{0,1},{1,0},{2,3},{3,2},{4,5},{5,4},{6,7},{7,6},{8,9},{9,8},{10,11... | collective-permute-start | bytes 393224 | tf_op jit(solution)/shard_map/ppermute | solution.py:349
  94.6 9.9 %collective-permute-start.17 = (bf16[32,2048]{1,0:T(8,128)(2,1)S(1)}, bf16[32,2048]{1,0:T(8,128)(2,1)S(1)}, u32[]{:S(2)}, u32[]{:S(2)}) collective-permute-start(bf16[32,2048]{1,0:T(8,128)(2,1)S(1)} %get-tuple-element.96), channel_id=1, source_target_pairs={{0,2},{1,3},{2,0},{3,1},{4,6},{5,7},{6,4},{7,5},{8,10},{9,11},{10,... | collective-permute-start | bytes 393224 | tf_op jit(solution)/shard_map/ppermute | solution.py:349
  95.3 9.9 %collective-permute-start.18 = (bf16[32,2048]{1,0:T(8,128)(2,1)S(1)}, bf16[32,2048]{1,0:T(8,128)(2,1)S(1)}, u32[]{:S(2)}, u32[]{:S(2)}) collective-permute-start(bf16[32,2048]{1,0:T(8,128)(2,1)S(1)} %get-tuple-element.97), channel_id=1, source_target_pairs={{0,3},{1,2},{2,1},{3,0},{4,7},{5,6},{6,5},{7,4},{8,11},{9,10},{10,... | collective-permute-start | bytes 393224 | tf_op jit(solution)/shard_map/ppermute | solution.py:349
  97.9 8.4 %collective-permute-start.20 = (bf16[32,2048]{1,0:T(8,128)(2,1)S(1)}, bf16[32,2048]{1,0:T(8,128)(2,1)S(1)}, u32[]{:S(2)}, u32[]{:S(2)}) collective-permute-start(bf16[32,2048]{1,0:T(8,128)(2,1)S(1)} %get-tuple-element.100), channel_id=1, source_target_pairs={{0,1},{1,0},{2,3},{3,2},{4,5},{5,4},{6,7},{7,6},{8,9},{9,8},{10,11... | collective-permute-start | bytes 393224 | tf_op jit(solution)/shard_map/ppermute | solution.py:349
  99.0 10.1 %collective-permute-start.21 = (bf16[32,2048]{1,0:T(8,128)(2,1)S(1)}, bf16[32,2048]{1,0:T(8,128)(2,1)S(1)}, u32[]{:S(2)}, u32[]{:S(2)}) collective-permute-start(bf16[32,2048]{1,0:T(8,128)(2,1)S(1)} %get-tuple-element.101), channel_id=1, source_target_pairs={{0,2},{1,3},{2,0},{3,1},{4,6},{5,7},{6,4},{7,5},{8,10},{9,11},{10,... | collective-permute-start | bytes 393224 | tf_op jit(solution)/shard_map/ppermute | solution.py:349
  100.3 10.0 %collective-permute-start.22 = (bf16[32,2048]{1,0:T(8,128)(2,1)S(1)}, bf16[32,2048]{1,0:T(8,128)(2,1)S(1)}, u32[]{:S(2)}, u32[]{:S(2)}) collective-permute-start(bf16[32,2048]{1,0:T(8,128)(2,1)S(1)} %get-tuple-element.102), channel_id=1, source_target_pairs={{0,3},{1,2},{2,1},{3,0},{4,7},{5,6},{6,5},{7,4},{8,11},{9,10},{10,... | collective-permute-start | bytes 393224 | tf_op jit(solution)/shard_map/ppermute | solution.py:349
  104.5 9.6 %collective-permute-start.6 = (bf16[32,1024]{1,0:T(8,128)(2,1)S(1)}, bf16[32,1024]{1,0:T(8,128)(2,1)S(1)}, u32[]{:S(2)}, u32[]{:S(2)}) collective-permute-start(bf16[32,1024]{1,0:T(8,128)(2,1)S(1)} %get-tuple-element.79), channel_id=1, source_target_pairs={{0,2},{1,3},{2,0},{3,1},{4,6},{5,7},{6,4},{7,5},{8,10},{9,11},{10,... | collective-permute-start | bytes 196616 | tf_op jit(solution)/shard_map/ppermute | solution.py:349
  105.1 9.0 %collective-permute-start.7 = (bf16[32,1024]{1,0:T(8,128)(2,1)S(1)}, bf16[32,1024]{1,0:T(8,128)(2,1)S(1)}, u32[]{:S(2)}, u32[]{:S(2)}) collective-permute-start(bf16[32,1024]{1,0:T(8,128)(2,1)S(1)} %get-tuple-element.80), channel_id=1, source_target_pairs={{0,3},{1,2},{2,1},{3,0},{4,7},{5,6},{6,5},{7,4},{8,11},{9,10},{10,... | collective-permute-start | bytes 196616 | tf_op jit(solution)/shard_map/ppermute | solution.py:349
  106.3 7.8 %collective-permute-start.1 = (bf16[32,1024]{1,0:T(8,128)(2,1)S(1)}, bf16[32,1024]{1,0:T(8,128)(2,1)S(1)}, u32[]{:S(2)}, u32[]{:S(2)}) collective-permute-start(bf16[32,1024]{1,0:T(8,128)(2,1)S(1)} %get-tuple-element.73), channel_id=1, source_target_pairs={{0,1},{1,0},{2,3},{3,2},{4,5},{5,4},{6,7},{7,6},{8,9},{9,8},{10,11... | collective-permute-start | bytes 196616 | tf_op jit(solution)/shard_map/ppermute | solution.py:349
  109.2 6.9 %collective-permute-start.2 = (bf16[32,1024]{1,0:T(8,128)(2,1)S(1)}, bf16[32,1024]{1,0:T(8,128)(2,1)S(1)}, u32[]{:S(2)}, u32[]{:S(2)}) collective-permute-start(bf16[32,1024]{1,0:T(8,128)(2,1)S(1)} %get-tuple-element.74), channel_id=1, source_target_pairs={{0,2},{1,3},{2,0},{3,1},{4,6},{5,7},{6,4},{7,5},{8,10},{9,11},{10,... | collective-permute-start | bytes 196616 | tf_op jit(solution)/shard_map/ppermute | solution.py:349
  110.3 5.8 %collective-permute-start.3 = (bf16[32,1024]{1,0:T(8,128)(2,1)S(1)}, bf16[32,1024]{1,0:T(8,128)(2,1)S(1)}, u32[]{:S(2)}, u32[]{:S(2)}) collective-permute-start(bf16[32,1024]{1,0:T(8,128)(2,1)S(1)} %get-tuple-element.75), channel_id=1, source_target_pairs={{0,3},{1,2},{2,1},{3,0},{4,7},{5,6},{6,5},{7,4},{8,11},{9,10},{10,... | collective-permute-start | bytes 196616 | tf_op jit(solution)/shard_map/ppermute | solution.py:349
  116.0 14.5 %copy-start.2 = (s32[8,512]{1,0:T(8,128)S(1)}, s32[8,512]{1,0:T(8,128)}, u32[]{:S(2)}) copy-start(s32[8,512]{1,0:T(8,128)} %get-tuple-element.70.key_hbm.key_ref) | copy-start | bytes 49156
where the time goes:
time: 132 us
  starting transfers between devices  59.1 us (45%)
  blocking collectives  36 us (27%)
  Pallas kernels  19.6 us (15%)
  waiting for transfers between devices  15.9 us (12%)
    all_to_all x2, blocking collectives, exchange(): return lax.all_to_all(value, ('dp', 'cent'), 0, 0, tiled=True)  36 us
    ppermute x8, starting transfers between devices, send(): return lax.ppermute(value, 'dp', [(i, shift(i, m)) for i in range(dp)])  35.7 us
    ppermute x24, starting transfers between devices, send(): return lax.ppermute(value, 'cent', [(j, j ^ e) for j in range(cent)])  20.5 us
    pallas_call x15, Pallas kernels, call(): pl.pallas_call(body, out_shape=outs, in_specs=[pl.BlockSpec(memory_space=...  19.6 us
    ppermute x24, waiting for transfers between devices, send(): return lax.ppermute(value, 'cent', [(j, j ^ e) for j in range(cent)])  12.1 us
    ppermute x3, starting transfers between devices, send(): return lax.ppermute(value, ('dp', 'cent'), pairs)  2.9 us
  transfers between devices with their start and end apart: 35, of which 11 were waited for; matrix products, arithmetic and copies ran while one was open for 0% of the time, Pallas kernels for 6%

commit v1 on v0

--- a/solution.py
+++ b/solution.py
@@ -113,7 +113,8 @@
     root = math.sqrt(width)
     far, direct, relayed, stages = plan()
     source = lambda m, e: back_shift(lax.axis_index("dp"), m) * cent + (lax.axis_index("cent") ^ e)
-    span = lambda f: (f[1] * width // f[2], (f[1] + 1) * width // f[2])
+    span = lambda f: (f[1] * width // 4, f[2] * width // 4)
+    size = lambda f: span(f)[1] - span(f)[0]
 
     def route(assigned_hbm, table_hbm, docs_hbm, far_ref, tag_ref, key_ref, *scratch):
         assigned_ref, table_ref, docs_ref, sems = scratch
@@ -128,21 +129,35 @@
         copies[0].wait()
         copies[1].wait()
         a = assigned_ref[...]
-        pick = (iota((clusters // LANES, docs), 0) == a // LANES).astype(jnp.float32)
-        lines = mm(table_ref[...].astype(jnp.float32), pick, ((0,), (0,)), HIGHEST)
+        pick = (iota((clusters // LANES, docs), 0) == a // LANES).astype(jnp.bfloat16)
+        digits, left = [], clusters - 1
+        while left:
+            digits.append((table_ref[...] >> (7 * len(digits))) & (LANES - 1))
+            left >>= 7
+        digits = [d.astype(jnp.float32).astype(jnp.bfloat16) for d in digits]
+        lines = mm(jnp.concatenate(digits, axis=1), pick, ((0,), (0,)))
+        value = lines[:LANES]
+        for n in range(1, len(digits)):
+            value = value + lines[n * LANES : (n + 1) * LANES] * float(LANES**n)
         slot = jnp.sum(
-            jnp.where(iota((LANES, docs), 0) == a % LANES, lines, 0.0), axis=0, keepdims=True
+            jnp.where(iota((LANES, docs), 0) == a % LANES, value, 0.0), axis=0, keepdims=True
         )
         owner = jnp.floor((slot + 0.5) * (1.0 / rows))
-        home = slot - owner * rows + 1.0
+        home = (slot - owner * rows).astype(jnp.int32) + 1
         owner = owner.astype(jnp.int32)
         here, side = lax.axis_index("dp"), lax.axis_index("cent")
         rel = relative(owner // cent, here) * cent + ((owner % cent) ^ side)
         which = iota((owners, docs), 0)
         mine = which == owner
         near = which // cent == owner // cent
-        earlier = (iota((docs, docs), 0) < iota((docs, docs), 1)).astype(jnp.bfloat16)
-        before = mm(mine.astype(jnp.bfloat16), earlier, ((1,), (0,)))
+        earlier = (iota((LANES, LANES), 0) < iota((LANES, LANES), 1)).astype(jnp.bfloat16)
+        marks = mine.astype(jnp.float32)
+        before, total = [], jnp.zeros((owners, 1), jnp.float32)
+        for lo in range(0, docs, LANES):
+            part = marks[:, lo : lo + LANES]
+            before.append(mm(part.astype(jnp.bfloat16), earlier, ((1,), (0,))) + total)
+            total = total + jnp.sum(part, axis=1, keepdims=True)
+        before = jnp.concatenate(before, axis=1)
         count = lambda m: jnp.sum(jnp.where(m, before, 0.0), axis=0, keepdims=True)
         rank = count(mine).astype(jnp.int32)
         row_rank = count(near).astype(jnp.int32)
@@ -151,11 +166,13 @@
         key_ref[0:1, :] = key
         key_ref[1:2, :] = row_key
         key_ref[2:3, :] = owner
-        at_rank = (iota((cap, docs), 0) == rank).astype(jnp.float32)
-        at_row = (iota((row_cap, docs), 0) == row_rank).astype(jnp.float32)
-        homes = mm(jnp.where(mine, home, 0.0), at_rank, ((1,), (1,)), HIGHEST)
-        inner = (key % group + 1).astype(jnp.float32)
-        inners = mm(jnp.where(near, inner, 0.0), at_row, ((1,), (1,)), HIGHEST)
+        spread = lambda m, v: jnp.where(m, v.astype(jnp.float32), 0.0).astype(jnp.bfloat16)
+        at_rank = (iota((cap, docs), 0) == rank).astype(jnp.bfloat16)
+        at_row = (iota((row_cap, docs), 0) == row_rank).astype(jnp.bfloat16)
+        homes = jnp.concatenate([spread(mine, home // LANES), spread(mine, home % LANES)], axis=0)
+        homes = mm(homes, at_rank, ((1,), (1,)))
+        homes = homes[:owners] * float(LANES) + homes[owners:]
+        inners = mm(spread(near, key % group + 1), at_row, ((1,), (1,)))
         tag_ref[...] = jnp.zeros((owners, 1, LANES), jnp.int32)
         tag_ref[:, 0, :cap] = homes.astype(jnp.int32)
         tag_ref[:, 0, cap : cap + row_cap] = inners.astype(jnp.int32)
@@ -207,6 +224,28 @@
 
         return body
 
+    def fill(x, parts, masks, arrays):
+        start = span(parts[0][0])[0] if len(masks) == 1 else 0
+        for part, refs in zip(parts, arrays):
+            for i, f in enumerate(part):
+                lo, hi = span(f)
+                for e in range(cent):
+                    at = (masks.index(f[0]) * cent + e) * cap
+                    x[at : at + cap, lo - start : hi - start] = refs[e][i * cap : (i + 1) * cap, :]
+
+    def partial(*refs):
+        parts = stages[-1][:-1]
+        refs = list(refs)
+        arrays = [[refs.pop(0) for _ in range(cent)] for _ in parts]
+        *lefts, acc_ref, x = refs
+        fill(x, parts, stage_masks(parts), arrays)
+        xn, base = x[...], 0
+        for left in lefts:
+            out = mm(left[:, : xn.shape[1]], xn, ((1,), (1,)))
+            acc_ref[base : base + out.shape[0], :] = out
+            base += out.shape[0]
+        acc_ref[base:, :] = mm(xn, xn, ((1,), (1,)))
+
     def make_owner(s):
         parts = stages[s]
         masks = stage_masks(parts)
@@ -216,21 +255,27 @@
         def body(*refs):
             refs = list(refs)
             take = lambda n: [refs.pop(0) for _ in range(n)]
-            arrays = [take(cent) for _ in parts]
+            arrays = [take(cent) for _ in (parts[-1:] if last else parts)]
             tag_ref, cent_ref, cent_inv_ref = take(3)
-            olds = [take(3) for _ in range(s)]
+            olds = [take(4) for _ in range(s)]
             tally = take(1)[0] if s else None
+            acc_ref = take(1)[0] if last else None
             if last:
                 score_ref, stat_ref, x = take(3)
             else:
-                x, col, line, tally_out = take(4)
+                x, col, line, own_ref, tally_out = take(5)
                 old_outs = take(s)
-            for part, refs_e in zip(parts, arrays):
-                for i, f in enumerate(part):
-                    lo, hi = span(f)
-                    for e in range(cent):
-                        at = (masks.index(f[0]) * cent + e) * cap
-                        x[at : at + cap, lo:hi] = refs_e[e][i * cap : (i + 1) * cap, :]
+            fill(x, parts[-1:] if last else parts, masks, arrays)
+            lane = slice(*span(parts[-1][0])) if last else slice(None)
+            base = [0]
+
+            def dots(left, right):
+                out = mm(left[:, lane], right, ((1,), (1,)))
+                if last:
+                    out = out + acc_ref[base[0] : base[0] + out.shape[0], :]
+                base[0] += out.shape[0]
+                return out
+
             tags = [
                 tag_ref[pl.ds(source(m, e), 1), 0, :cap] for m in masks for e in range(cent)
             ]
@@ -257,7 +302,9 @@
             else:
                 counts = [tally[:, i : i + 1] for i in range(3)]
             xn = x[...]
-            own_gram = mm(xn, xn, ((1,), (1,)))
+            cross = dots(cent_ref, xn)
+            grams = [dots(old[0], xn) for old in olds]
+            own_gram = mm(xn, xn, ((1,), (1,))) + (acc_ref[base[0] :, :] if last else 0.0)
             cols, lines = [], []
             for i in range(0, fresh, LANES):
                 diag = jnp.where(eye, own_gram[i : i + LANES, i : i + LANES], 0.0)
@@ -266,7 +313,6 @@
             tag_col = to_col(tag)
             inv_col = jnp.concatenate(cols, axis=0)
             inv = jnp.concatenate(lines, axis=1)
-            cross = mm(cent_ref[...], xn, ((1,), (1,)))
             own = (iota((rows, fresh), 0) + 1).astype(jnp.float32) == tag
             sim = jnp.sum(jnp.where(own, cross * cent_inv, 0.0), axis=0, keepdims=True) * inv
             add = lambda v: jnp.sum(jnp.where(own, v, 0.0), axis=1, keepdims=True)
@@ -274,8 +320,7 @@
             same = (tag_col == tag) & (iota((fresh, fresh), 0) != iota((fresh, fresh), 1))
             best = jnp.max(jnp.where(same, own_gram * inv_col, 0.0), axis=0, keepdims=True)
             old_best = []
-            for x_old, col_old, line_old in olds:
-                gram = mm(x_old[...], xn, ((1,), (1,)))
+            for gram, (_, col_old, line_old, _) in zip(grams, olds):
                 same = col_old[:, 0:1] == tag
                 up = jnp.max(
                     jnp.where(same, gram * col_old[:, 1:2], 0.0), axis=0, keepdims=True
@@ -290,23 +335,34 @@
                     line[i : i + 1, :] = v
                 for i, v in enumerate(counts):
                     tally_out[:, i : i + 1] = v
-                for ref, (_, _, line_old), v in zip(old_outs, olds, old_best):
+                own_ref[...] = own.astype(jnp.bfloat16)
+                for ref, (_, _, line_old, _), v in zip(old_outs, olds, old_best):
                     ref[0:3, :] = line_old[0:3, :]
                     ref[3:4, :] = v
                 return
-            floor = jnp.maximum(counts[0], 1.0)
-            mean = counts[1] / floor
-            var = jnp.maximum(counts[2] / floor - mean * mean, 0.0)
-            spread = 1.0 / jnp.sqrt(var + 1.0 / width)
-            for i, v in enumerate(counts):
-                stat_ref[i : i + 1, :] = to_row(v)
-            facts = [(l[0:1, :], l[1:2, :], l[2:3, :], b) for (_, _, l), b in zip(olds, old_best)]
-            facts.append((tag, inv, sim, best))
-            for parts_s, (tag, inv, sim, best) in zip(stages, facts):
+            count, s1, s2 = [to_row(v) for v in counts]
+            for i, v in enumerate((count, s1, s2)):
+                stat_ref[i : i + 1, :] = v
+            floor = jnp.maximum(count, 1.0)
+            mean = s1 / floor
+            var = jnp.maximum(s2 / floor - mean * mean, 0.0)
+            terms = []
+            for v in (mean, 1.0 / jnp.sqrt(var + 1.0 / width)):
+                for _ in range(3):
+                    terms.append(v.astype(jnp.bfloat16).astype(jnp.float32))
+                    v = v - terms[-1]
+            table = jnp.zeros((8, rows), jnp.float32)
+            for i, v in enumerate(terms):
+                table = jnp.where(iota((8, rows), 0) == i, v, table)
+            table = table.astype(jnp.bfloat16)
+            facts = [(l[1:2, :], l[2:3, :], v, o) for (_, _, l, o), v in zip(olds, old_best)]
+            facts.append((inv, sim, best, own.astype(jnp.bfloat16)))
+            for parts_s, (inv, sim, best, own) in zip(stages, facts):
                 order_s = stage_masks(parts_s)
-                own = (iota((rows, tag.shape[1]), 0) + 1).astype(jnp.float32) == tag
-                pick = lambda v: jnp.sum(jnp.where(own, v, 0.0), axis=0, keepdims=True)
-                score = (pick(mean) - sim) * pick(spread)
+                got = mm(table, own[...], ((1,), (0,)))
+                mean_d = got[0:1, :] + got[1:2, :] + got[2:3, :]
+                spread_d = got[3:4, :] + got[4:5, :] + got[5:6, :]
+                score = (mean_d - sim) * spread_d
                 red = best * inv * root
                 for b in range(len(order_s) * cent):
                     part = slice(b * cap, (b + 1) * cap)
@@ -316,7 +372,8 @@
 
         return body
 
-    def unpack(score_ref, key_ref, out_ref, red_ref):
+    def unpack(score_ref, key_ref, stat_ref, out_ref, red_ref, stat_out):
+        stat_out[...] = stat_ref[...]
         key = key_ref[0:1, :]
         pick = (iota((owners, docs), 0) == key_ref[2:3, :]).astype(jnp.float32)
         got = mm(score_ref[:, 0, :], pick, ((0,), (0,)), HIGHEST)
@@ -368,52 +425,61 @@
             held,
             pltpu.SemaphoreType.DMA((3,)),
         ],
-        mib=63,
+        mib=62,
         space=pl.ANY,
     )
     tags = exchange(tags)
     got = call(
         pack,
         (key, documents),
-        [bf16(row_cap, width // f[2]) for f in far[1:]]
+        [bf16(row_cap, size(f)) for f in far[1:]]
         + [bf16(cap, width)] * (len(direct) * cent),
         2 * len(far) * row_cap * docs * width,
         [pltpu.VMEM((8, docs), jnp.int32), held, pltpu.SemaphoreType.DMA((2,))],
-        mib=63,
+        mib=62,
         space=pl.ANY,
     )
     sent = {f: send(v, f[0], 0) for f, v in zip(far, [first, *got])}
     arrays = {}
     for n, m in enumerate(direct):
         near = got[len(far) - 1 + n * cent : len(far) - 1 + (n + 1) * cent]
-        arrays[((m, 0, 1),)] = [send(v, m, e) for e, v in enumerate(near)]
+        arrays[((m, 0, 4),)] = [send(v, m, e) for e, v in enumerate(near)]
     for part in relayed:
-        size = width // part[0][2]
+        wide = size(part[0])
         hop = call(
             make_relay(part),
             (tags, *[sent[f] for f in part]),
-            [bf16(len(part) * cap, size)] * cent,
-            2 * len(part) * group * row_cap * size,
+            [bf16(len(part) * cap, wide)] * cent,
+            2 * len(part) * group * row_cap * wide,
         )
         arrays[part] = [send(hop[e], 0, e) for e in range(cent)]
     kept, cent_inv = call(norms, (centroids,), [bf16(rows, width), f32(rows, 1)], 2 * rows * width)
     olds, tally = [], None
     for s, parts in enumerate(stages):
         fresh = len(stage_masks(parts)) * group
-        ins = [b for part in parts for b in arrays[part]] + [tags, kept, cent_inv]
+        last = s == len(stages) - 1
+        ins = [b for part in (parts[-1:] if last else parts) for b in arrays[part]]
+        ins += [tags, kept, cent_inv]
         ins += [v for old in olds for v in old] + ([tally] if s else [])
-        flops = 2 * fresh * (rows + fresh + sum(o[0].shape[0] for o in olds)) * width
-        if s < len(stages) - 1:
-            outs = [bf16(fresh, width), f32(fresh, 2), f32(4, fresh), f32(rows, 3)]
-            outs += [f32(*o[2].shape) for o in olds]
-            x, col, line, tally, *lines = call(make_owner(s), ins, outs, flops)
-            olds = [(o[0], o[1], l) for o, l in zip(olds, lines)] + [(x, col, line)]
+        many = rows + fresh + sum(o[0].shape[0] for o in olds)
+        flops = 2 * fresh * many * width
+        if not last:
+            outs = [bf16(fresh, width), f32(fresh, 2), f32(4, fresh), bf16(rows, fresh)]
+            outs += [f32(rows, 3)] + [f32(*o[2].shape) for o in olds]
+            x, col, line, own, tally, *lines = call(make_owner(s), ins, outs, flops)
+            olds = [(o[0], o[1], l, o[3]) for o, l in zip(olds, lines)] + [(x, col, line, own)]
         else:
-            scratch = [pltpu.VMEM((fresh, width), jnp.bfloat16)]
+            early = [b for part in parts[:-1] for b in arrays[part]] + [kept] + [o[0] for o in olds]
+            wide = span(parts[-1][0])[0]
+            (acc,) = call(
+                partial, early, [f32(many, fresh)], flops, [pltpu.VMEM((fresh, wide), jnp.bfloat16)]
+            )
+            scratch = [pltpu.VMEM((fresh, width - wide), jnp.bfloat16)]
             outs = [f32(owners, 1, 2 * cap), f32(3, rows)]
-            scores, stats = call(make_owner(s), ins, outs, flops, scratch)
+            scores, stats = call(make_owner(s), ins + [acc], outs, flops // 4, scratch)
     back = exchange(scores)
-    proto, red = call(unpack, (back, key), [f32(1, docs)] * 2, 1 << 20)
+    outs = [f32(1, docs), f32(1, docs), f32(3, rows)]
+    proto, red, stats = call(unpack, (back, key, stats), outs, 1 << 20)
     return proto.reshape(docs), red.reshape(docs), stats
 
 
@@ -425,16 +491,16 @@
 
 
 def plan():
-    whole = lambda *masks: tuple((m, 0, 1) for m in masks)
-    lo, hi = (5, 0, 2), (5, 1, 2)
-    far = [f[0] for f in map(whole, (4, 2, 6, 3, 7))] + [lo, hi]
+    whole = lambda *masks: tuple((m, 0, 4) for m in masks)
+    cuts = [(5, 0, 2), (5, 2, 4)]
+    far = [f[0] for f in map(whole, (4, 2, 6, 3, 7))] + cuts
     relayed = [(f,) for f in far]
     direct = [0, 1]
     stages = [
         [whole(0), whole(1)],
         [whole(4), whole(2), whole(6)],
         [whole(3), whole(7)],
-        [(lo,), (hi,)],
+        [(f,) for f in cuts],
     ]
     return far, direct, relayed, stages
 

time: 132 us -> 129 us (0.977)
  starting transfers between devices: 59.1 us -> 43.1 us
  blocking collectives: 36 us -> 43.7 us
  waiting for transfers between devices: 15.9 us -> 20.3 us
    ppermute x8, starting transfers between devices: 35.7 us -> 20.9 us  [send(): return lax.ppermute(value, 'dp', [(i, shift(i, m)) for i in range(dp)])]
    all_to_all x2, blocking collectives: 36 us -> 43.7 us  [exchange(): return lax.all_to_all(value, ('dp', 'cent'), 0, 0, tiled=True)]
    ppermute x24, starting transfers between devices: 20.5 us -> 16.8 us  [send(): return lax.ppermute(value, 'cent', [(j, j ^ e) for j in range(cent)])]
    ppermute x3, waiting for transfers between devices: 1.33 us -> 4.18 us  [send(): return lax.ppermute(value, ('dp', 'cent'), pairs)]
    ppermute x3, starting transfers between devices: 2.9 us -> 5.48 us  [send(): return lax.ppermute(value, ('dp', 'cent'), pairs)]
    ppermute x24, waiting for transfers between devices: 12.1 us -> 14.4 us  [send(): return lax.ppermute(value, 'cent', [(j, j ^ e) for j in range(cent)])]
    pallas_call x15 -> x16, Pallas kernels: 19.6 us -> 20.4 us  [call(): pl.pallas_call(body, out_shape=outs, in_specs=[pl.BlockSpec(memory_space=...]
  transfers between devices with their start and end apart: 35 -> 35, of which waited for: 11 -> 14; matrix products, arithmetic and copies ran while one was open for 0% -> 0% of each run, Pallas kernels for 6% -> 8%
where the time goes in v1:
time: 129 us; the launch traced here: 128 us
  blocking collectives  43.7 us (34%)
  starting transfers between devices  43.1 us (33%)
  Pallas kernels  20.4 us (16%)
  waiting for transfers between devices  20.3 us (16%)
    all_to_all x2, blocking collectives, exchange(): return lax.all_to_all(value, ('dp', 'cent'), 0, 0, tiled=True)  43.7 us
    ppermute x8, starting transfers between devices, send(): return lax.ppermute(value, 'dp', [(i, shift(i, m)) for i in range(dp)])  20.9 us
    pallas_call x16, Pallas kernels, call(): pl.pallas_call(body, out_shape=outs, in_specs=[pl.BlockSpec(memory_space=...  20.4 us
    ppermute x24, starting transfers between devices, send(): return lax.ppermute(value, 'cent', [(j, j ^ e) for j in range(cent)])  16.8 us
    ppermute x24, waiting for transfers between devices, send(): return lax.ppermute(value, 'cent', [(j, j ^ e) for j in range(cent)])  14.4 us
    ppermute x3, starting transfers between devices, send(): return lax.ppermute(value, ('dp', 'cent'), pairs)  5.48 us
    ppermute x3, waiting for transfers between devices, send(): return lax.ppermute(value, ('dp', 'cent'), pairs)  4.18 us
  transfers between devices with their start and end apart: 35, of which 14 were waited for; matrix products, arithmetic and copies ran while one was open for 0% of the time, Pallas kernels for 8%

profile of v1, /device:TPU:0, one launch (start us, length us, event | category | flops | bytes accessed | tf_op | source)
XLA Modules:
  0.0 128.4 jit_solution(14055865427431536689)
XLA Ops:
  0.6 2.9 %shard_map.67 = (bf16[80,2048]{1,0:T(8,128)(2,1)}, s32[32,1,128]{2,1,0:T(1,128)}, s32[8,512]{1,0:T(8,128)}) custom-call(s32[1,512]{1,0:T(1,128)} %bitcast.5, s32[96,128]{1,0:T(8,128)} %bitcast.4, bf16[512,2048]{1,0:T(8,128)(2,1)} %docs_hbm.3), custom_call_target="tpu_custom_call" | custom-call | flops 167772160 | bytes 1048576 | tf_op jit(solution)/shard_map/pallas_call | solution.py:390
  3.5 4.7 %shard_map.68 = (bf16[80,2048]{1,0:T(8,128)(2,1)}, bf16[80,2048]{1,0:T(8,128)(2,1)}, bf16[80,2048]{1,0:T(8,128)(2,1)}, bf16[80,2048]{1,0:T(8,128)(2,1)}, bf16[80...) custom-call(s32[8,512]{1,0:T(8,128)} %get-tuple-element.74.key_hbm.k, ...), custom_call_target="tpu_custom_call" | custom-call | flops 1174405120 | bytes 1048576 | tf_op jit(solution)/shard_map/pallas_call | solution.py:390
  8.2 3.4 %collective-permute-start.10 = (bf16[32,2048]{1,0:T(8,128)(2,1)}, bf16[32,2048]{1,0:T(8,128)(2,1)S(1)}, u32[]{:S(2)}, u32[]{:S(2)}) collective-permute-start(bf16[32,2048]{1,0:T(8,128)(2,1)} %get-tuple-element.89), channel_id=1, source_target_pairs={{0,7},{1,6},{2,5},{3,4},{4,3},{5,2},{6,1},{7,0},{8,15},{9,14},{10,... | collective-permute-start | bytes 393224 | tf_op jit(solution)/shard_map/ppermute | solution.py:410
  11.7 0.7 collective-permute-start.4
  12.3 0.5 collective-permute-start.5
  12.8 0.8 collective-permute-start.6
  13.7 1.6 %collective-permute-start.23 = (bf16[80,2048]{1,0:T(8,128)(2,1)}, bf16[80,2048]{1,0:T(8,128)(2,1)S(1)}, u32[]{:S(2)}, u32[]{:S(2)}) collective-permute-start(bf16[80,2048]{1,0:T(8,128)(2,1)} %get-tuple-element.107), channel_id=1, source_target_pairs={{0,8},{4,12},{8,24},{12,28},{16,0},{20,4},{24,16},{28,20},{1,9},{5... | collective-permute-start | bytes 983048 | tf_op jit(solution)/shard_map/ppermute | solution.py:404
  15.3 0.6 collective-permute-done.10.refs_7_
  15.9 3.4 %collective-permute-start.27 = (bf16[80,2048]{1,0:T(8,128)(2,1)}, bf16[80,2048]{1,0:T(8,128)(2,1)S(1)}, u32[]{:S(2)}, u32[]{:S(2)}) collective-permute-start(bf16[80,2048]{1,0:T(8,128)(2,1)} %get-tuple-element.112), channel_id=1, source_target_pairs={{0,16},{4,20},{8,0},{12,4},{16,24},{20,28},{24,8},{28,12},{1,17},{... | collective-permute-start | bytes 983048 | tf_op jit(solution)/shard_map/ppermute | solution.py:404
  19.3 1.6 %collective-permute-start.7 = (bf16[32,2048]{1,0:T(8,128)(2,1)}, bf16[32,2048]{1,0:T(8,128)(2,1)S(1)}, u32[]{:S(2)}, u32[]{:S(2)}) collective-permute-start(bf16[32,2048]{1,0:T(8,128)(2,1)} %get-tuple-element.86), channel_id=1, source_target_pairs={{0,4},{4,0},{8,12},{12,8},{16,20},{20,16},{24,28},{28,24},{1,5},{5... | collective-permute-start | bytes 393224 | tf_op jit(solution)/shard_map/ppermute | solution.py:404
  20.8 0.6 collective-permute-done.6.refs_3_
  21.4 2.1 %collective-permute-start.9 = (bf16[32,2048]{1,0:T(8,128)(2,1)}, bf16[32,2048]{1,0:T(8,128)(2,1)S(1)}, u32[]{:S(2)}, u32[]{:S(2)}) collective-permute-start(bf16[32,2048]{1,0:T(8,128)(2,1)} %get-tuple-element.88), channel_id=1, source_target_pairs={{0,6},{1,7},{2,4},{3,5},{4,2},{5,3},{6,0},{7,1},{8,14},{9,15},{10,... | collective-permute-start | bytes 393224 | tf_op jit(solution)/shard_map/ppermute | solution.py:410
  23.5 1.7 %collective-permute-done.7.refs_4_ = bf16[32,2048]{1,0:T(8,128)(2,1)S(1)} collective-permute-done((bf16[32,2048]{1,0:T(8,128)(2,1)}, bf16[32,2048]{1,0:T(8,128)(2,1)S(1)}, u32[]{:S(2)}, u32[]{:S(2)}) %collective-permute-start.7) | collective-permute-done | bytes 131104 | tf_op jit(solution)/shard_map/ppermute | solution.py:404
  25.2 1.7 %collective-permute-start.19 = (bf16[80,2048]{1,0:T(8,128)(2,1)S(1)}, bf16[80,2048]{1,0:T(8,128)(2,1)S(1)}, u32[]{:S(2)}, u32[]{:S(2)}) collective-permute-start(bf16[80,2048]{1,0:T(8,128)(2,1)S(1)} %copy-done.4), channel_id=1, source_target_pairs={{0,24},{4,28},{8,16},{12,20},{16,8},{20,12},{24,0},{28,4},{1,25},{... | collective-permute-start | bytes 983048 | tf_op jit(solution)/shard_map/ppermute | solution.py:404
  26.8 1.0 collective-permute-done.8.refs_5_
  27.9 0.9 collective-permute-start.11
  28.8 2.5 %collective-permute-done.9.refs_6_ = bf16[32,2048]{1,0:T(8,128)(2,1)S(1)} collective-permute-done((bf16[32,2048]{1,0:T(8,128)(2,1)}, bf16[32,2048]{1,0:T(8,128)(2,1)S(1)}, u32[]{:S(2)}, u32[]{:S(2)}) %collective-permute-start.9) | collective-permute-done | bytes 131104 | tf_op jit(solution)/shard_map/ppermute | solution.py:410
  31.3 2.5 %collective-permute-start.15 = (bf16[80,2048]{1,0:T(8,128)(2,1)}, bf16[80,2048]{1,0:T(8,128)(2,1)S(1)}, u32[]{:S(2)}, u32[]{:S(2)}) collective-permute-start(bf16[80,2048]{1,0:T(8,128)(2,1)} %get-tuple-element.97), channel_id=1, source_target_pairs={{0,20},{4,16},{8,4},{12,0},{16,28},{20,24},{24,12},{28,8},{1,21},{... | collective-permute-start | bytes 983048 | tf_op jit(solution)/shard_map/ppermute | solution.py:404
  33.8 9.2 %collective-permute-start.31 = (bf16[80,1024]{1,0:T(8,128)(2,1)}, bf16[80,1024]{1,0:T(8,128)(2,1)S(1)}, u32[]{:S(2)}, u32[]{:S(2)}) collective-permute-start(bf16[80,1024]{1,0:T(8,128)(2,1)} %get-tuple-element.133), channel_id=1, source_target_pairs={{0,28},{4,24},{8,20},{12,16},{16,12},{20,8},{24,4},{28,0},{1,29},{... | collective-permute-start | bytes 491528 | tf_op jit(solution)/shard_map/ppermute | solution.py:404
  43.1 32.7 %all_to_all.10.tag_ref.refs_8_.refs_12_.refs_4_ = s32[32,1,128]{2,1,0:T(1,128)S(1)} all-to-all(s32[32,1,128]{2,1,0:T(1,128)S(1)} %copy-done.3), channel_id=1, replica_groups=mesh['dp'=8,'cent'=4] {'dp','cent'}, dimensions={0} | all-to-all | bytes 32768 | tf_op jit(solution)/shard_map/all_to_all | solution.py:413
  76.6 1.5 %collective-permute-start.25 = (bf16[32,2048]{1,0:T(8,128)(2,1)S(1)}, bf16[32,2048]{1,0:T(8,128)(2,1)S(1)}, u32[]{:S(2)}, u32[]{:S(2)}) collective-permute-start(bf16[32,2048]{1,0:T(8,128)(2,1)S(1)} %get-tuple-element.110), channel_id=1, source_target_pairs={{0,2},{1,3},{2,0},{3,1},{4,6},{5,7},{6,4},{7,5},{8,10},{9,11},{10,... | collective-permute-start | bytes 393224 | tf_op jit(solution)/shard_map/ppermute | solution.py:406
  78.8 1.4 %collective-permute-start.29 = (bf16[32,2048]{1,0:T(8,128)(2,1)S(1)}, bf16[32,2048]{1,0:T(8,128)(2,1)S(1)}, u32[]{:S(2)}, u32[]{:S(2)}) collective-permute-start(bf16[32,2048]{1,0:T(8,128)(2,1)S(1)} %get-tuple-element.115), channel_id=1, source_target_pairs={{0,2},{1,3},{2,0},{3,1},{4,6},{5,7},{6,4},{7,5},{8,10},{9,11},{10,... | collective-permute-start | bytes 393224 | tf_op jit(solution)/shard_map/ppermute | solution.py:406
  81.1 1.9 %collective-permute-done.25.refs_6_ = bf16[32,2048]{1,0:T(8,128)(2,1)S(1)} collective-permute-done((bf16[32,2048]{1,0:T(8,128)(2,1)S(1)}, bf16[32,2048]{1,0:T(8,128)(2,1)S(1)}, u32[]{:S(2)}, u32[]{:S(2)}) %collective-permute-start.25) | collective-permute-done | bytes 131104 | tf_op jit(solution)/shard_map/ppermute | solution.py:406
  83.1 1.8 %collective-permute-done.26.refs_7_ = bf16[32,2048]{1,0:T(8,128)(2,1)S(1)} collective-permute-done((bf16[32,2048]{1,0:T(8,128)(2,1)S(1)}, bf16[32,2048]{1,0:T(8,128)(2,1)S(1)}, u32[]{:S(2)}, u32[]{:S(2)}) %collective-permute-start.26) | collective-permute-done | bytes 131104 | tf_op jit(solution)/shard_map/ppermute | solution.py:406
  84.8 1.4 %collective-permute-start.21 = (bf16[32,2048]{1,0:T(8,128)(2,1)S(1)}, bf16[32,2048]{1,0:T(8,128)(2,1)S(1)}, u32[]{:S(2)}, u32[]{:S(2)}) collective-permute-start(bf16[32,2048]{1,0:T(8,128)(2,1)S(1)} %get-tuple-element.105), channel_id=1, source_target_pairs={{0,2},{1,3},{2,0},{3,1},{4,6},{5,7},{6,4},{7,5},{8,10},{9,11},{10,... | collective-permute-start | bytes 393224 | tf_op jit(solution)/shard_map/ppermute | solution.py:406
  86.2 0.8 collective-permute-start.22
  87.0 1.6 %collective-permute-done.29.refs_10_ = bf16[32,2048]{1,0:T(8,128)(2,1)S(1)} collective-permute-done((bf16[32,2048]{1,0:T(8,128)(2,1)S(1)}, bf16[32,2048]{1,0:T(8,128)(2,1)S(1)}, u32[]{:S(2)}, u32[]{:S(2)}) %collective-permute-start.29) | collective-permute-done | bytes 131104 | tf_op jit(solution)/shard_map/ppermute | solution.py:406
  88.7 0.4 shard_map.70
  89.1 1.3 shard_map.71
  91.3 1.5 %collective-permute-start.13 = (bf16[32,2048]{1,0:T(8,128)(2,1)S(1)}, bf16[32,2048]{1,0:T(8,128)(2,1)S(1)}, u32[]{:S(2)}, u32[]{:S(2)}) collective-permute-start(bf16[32,2048]{1,0:T(8,128)(2,1)S(1)} %get-tuple-element.95), channel_id=1, source_target_pairs={{0,2},{1,3},{2,0},{3,1},{4,6},{5,7},{6,4},{7,5},{8,10},{9,11},{10,... | collective-permute-start | bytes 393224 | tf_op jit(solution)/shard_map/ppermute | solution.py:406
  92.8 0.4 collective-permute-start.14
  93.2 1.1 collective-permute-done.21.refs_2_
  94.3 1.8 %collective-permute-done.22.refs_3_ = bf16[32,2048]{1,0:T(8,128)(2,1)S(1)} collective-permute-done((bf16[32,2048]{1,0:T(8,128)(2,1)S(1)}, bf16[32,2048]{1,0:T(8,128)(2,1)S(1)}, u32[]{:S(2)}, u32[]{:S(2)}) %collective-permute-start.22) | collective-permute-done | bytes 131104 | tf_op jit(solution)/shard_map/ppermute | solution.py:406
  96.1 1.4 %collective-permute-start.17 = (bf16[32,2048]{1,0:T(8,128)(2,1)S(1)}, bf16[32,2048]{1,0:T(8,128)(2,1)S(1)}, u32[]{:S(2)}, u32[]{:S(2)}) collective-permute-start(bf16[32,2048]{1,0:T(8,128)(2,1)S(1)} %get-tuple-element.100), channel_id=1, source_target_pairs={{0,2},{1,3},{2,0},{3,1},{4,6},{5,7},{6,4},{7,5},{8,10},{9,11},{10,... | collective-permute-start | bytes 393224 | tf_op jit(solution)/shard_map/ppermute | solution.py:406
  97.5 0.8 collective-permute-start.18
  98.3 3.1 %shard_map.77 = (bf16[384,2048]{1,0:T(8,128)(2,1)S(1)}, f32[384,2]{1,0:T(8,128)S(1)}, f32[4,384]{1,0:T(4,128)S(1)}, bf16[384,384]{1,0:T(8,128)(2,1)S(1)}, f32[384,3]{1,0:T(8,128)S(1)}, /*index=5*/f32[4,256]{1,0:T(4,128)S(1)}) custom-call(bf16[32,2048]{1,0:T(8,128)(2,1)S(1)} %get-tuple-element.103.refs_0_, ...), custom_call_target="tpu_custom_call" | custom-call | flops 1610612736 | bytes 1048576 | tf_op jit(solution)/shard_map/pallas_call | solution.py:390
  101.7 1.4 %collective-permute-start.33 = (bf16[32,1024]{1,0:T(8,128)(2,1)S(1)}, bf16[32,1024]{1,0:T(8,128)(2,1)S(1)}, u32[]{:S(2)}, u32[]{:S(2)}) collective-permute-start(bf16[32,1024]{1,0:T(8,128)(2,1)S(1)} %get-tuple-element.136), channel_id=1, source_target_pairs={{0,2},{1,3},{2,0},{3,1},{4,6},{5,7},{6,4},{7,5},{8,10},{9,11},{10,... | collective-permute-start | bytes 196616 | tf_op jit(solution)/shard_map/ppermute | solution.py:406
  103.1 0.8 collective-permute-start.34
  103.9 1.6 %collective-permute-done.17.refs_6_ = bf16[32,2048]{1,0:T(8,128)(2,1)S(1)} collective-permute-done((bf16[32,2048]{1,0:T(8,128)(2,1)S(1)}, bf16[32,2048]{1,0:T(8,128)(2,1)S(1)}, u32[]{:S(2)}, u32[]{:S(2)}) %collective-permute-start.17) | collective-permute-done | bytes 131104 | tf_op jit(solution)/shard_map/ppermute | solution.py:406
  105.5 1.8 %collective-permute-done.18.refs_7_ = bf16[32,2048]{1,0:T(8,128)(2,1)S(1)} collective-permute-done((bf16[32,2048]{1,0:T(8,128)(2,1)S(1)}, bf16[32,2048]{1,0:T(8,128)(2,1)S(1)}, u32[]{:S(2)}, u32[]{:S(2)}) %collective-permute-start.18) | collective-permute-done | bytes 131104 | tf_op jit(solution)/shard_map/ppermute | solution.py:406
  107.3 1.4 %collective-permute-start.2 = (bf16[32,1024]{1,0:T(8,128)(2,1)S(1)}, bf16[32,1024]{1,0:T(8,128)(2,1)S(1)}, u32[]{:S(2)}, u32[]{:S(2)}) collective-permute-start(bf16[32,1024]{1,0:T(8,128)(2,1)S(1)} %get-tuple-element.78), channel_id=1, source_target_pairs={{0,2},{1,3},{2,0},{3,1},{4,6},{5,7},{6,4},{7,5},{8,10},{9,11},{10,... | collective-permute-start | bytes 196616 | tf_op jit(solution)/shard_map/ppermute | solution.py:406
  108.7 2.2 %shard_map.78 = (bf16[256,2048]{1,0:T(8,128)(2,1)S(1)}, f32[256,2]{1,0:T(8,128)S(1)}, f32[4,256]{1,0:T(4,128)S(1)}, bf16[384,256]{1,0:T(8,128)(2,1)S(1)}, f32[38...) custom-call(bf16[32,2048]{1,0:T(8,128)(2,1)S(1)} %get-tuple-element.93.refs_0_, ...), custom_call_target="tpu_custom_call" | custom-call | flops 1342177280 | bytes 1048576 | tf_op jit(solution)/shard_map/pallas_call | solution.py:390
  110.9 0.9 collective-permute-start.3
  111.8 0.9 shard_map.80.refs_20_
  112.7 1.9 %collective-permute-done.3.refs_3_ = bf16[32,1024]{1,0:T(8,128)(2,1)S(1)} collective-permute-done((bf16[32,1024]{1,0:T(8,128)(2,1)S(1)}, bf16[32,1024]{1,0:T(8,128)(2,1)S(1)}, u32[]{:S(2)}, u32[]{:S(2)}) %collective-permute-start.3) | collective-permute-done | bytes 65568 | tf_op jit(solution)/shard_map/ppermute | solution.py:406
  114.7 1.8 %shard_map.81 = (f32[32,1,64]{2,1,0:T(1,128)S(1)}, f32[3,384]{1,0:T(4,128)S(1)}) custom-call(bf16[32,1024]{1,0:T(8,128)(2,1)S(1)} %get-tuple-element.76.refs_0_, bf16[32,1024]{1,0:T(8,128)(2,1)S(1)} %collective-permute-done.1.refs_1_, bf16[32,1024]{1,0:T(8,128)(2,1)S(1)} %collective-permute-done.2.refs_2_, ...), custom_call_target="tpu_custom_call" | custom-call | flops 184549376 | bytes 1048576 | tf_op jit(solution)/shard_map/pallas_call | solution.py:390
  116.4 11.0 %all_to_all.11.score_ref = f32[32,1,64]{2,1,0:T(1,128)S(1)} all-to-all(f32[32,1,64]{2,1,0:T(1,128)S(1)} %get-tuple-element.138), channel_id=1, replica_groups=mesh['dp'=8,'cent'=4] {'dp','cent'}, dimensions={0} | all-to-all | bytes 16384 | tf_op jit(solution)/shard_map/all_to_all | solution.py:413
  127.5 0.9 shard_map.82
  (50 shorter events, 3.6 us)
Async XLA Ops:
  3.5 21.7 %copy-start.4 = (bf16[80,2048]{1,0:T(8,128)(2,1)S(1)}, bf16[80,2048]{1,0:T(8,128)(2,1)}, u32[]{:S(2)}) copy-start(bf16[80,2048]{1,0:T(8,128)(2,1)} %get-tuple-element.102) | copy-start | bytes 983044
  3.5 39.6 %copy-start.3 = (s32[32,1,128]{2,1,0:T(1,128)S(1)}, s32[32,1,128]{2,1,0:T(1,128)}, u32[]{:S(2)}) copy-start(s32[32,1,128]{2,1,0:T(1,128)} %get-tuple-element.73) | copy-start | bytes 49156
  3.5 85.2 %copy-start = (bf16[384,2048]{1,0:T(8,128)(2,1)S(1)}, bf16[384,2048]{1,0:T(8,128)(2,1)}, u32[]{:S(2)}) copy-start(bf16[384,2048]{1,0:T(8,128)(2,1)} %cent_ref.1) | copy-start | bytes 4718596
  8.2 80.9 %copy-start.1 = (bf16[32,2048]{1,0:T(8,128)(2,1)S(1)}, bf16[32,2048]{1,0:T(8,128)(2,1)}, u32[]{:S(2)}) copy-start(bf16[32,2048]{1,0:T(8,128)(2,1)} %get-tuple-element.82.refs_0_) | copy-start | bytes 393220
  8.2 7.7 %collective-permute-start.10 = (bf16[32,2048]{1,0:T(8,128)(2,1)}, bf16[32,2048]{1,0:T(8,128)(2,1)S(1)}, u32[]{:S(2)}, u32[]{:S(2)}) collective-permute-start(bf16[32,2048]{1,0:T(8,128)(2,1)} %get-tuple-element.89), channel_id=1, source_target_pairs={{0,7},{1,6},{2,5},{3,4},{4,3},{5,2},{6,1},{7,0},{8,15},{9,14},{10,... | collective-permute-start | bytes 393224 | tf_op jit(solution)/shard_map/ppermute | solution.py:410
  11.7 7.6 %collective-permute-start.4 = (bf16[32,2048]{1,0:T(8,128)(2,1)}, bf16[32,2048]{1,0:T(8,128)(2,1)S(1)}, u32[]{:S(2)}, u32[]{:S(2)}) collective-permute-start(bf16[32,2048]{1,0:T(8,128)(2,1)} %get-tuple-element.83), channel_id=1, source_target_pairs={{0,1},{1,0},{2,3},{3,2},{4,5},{5,4},{6,7},{7,6},{8,9},{9,8},{10,11... | collective-permute-start | bytes 393224 | tf_op jit(solution)/shard_map/ppermute | solution.py:406
  12.3 8.5 %collective-permute-start.5 = (bf16[32,2048]{1,0:T(8,128)(2,1)}, bf16[32,2048]{1,0:T(8,128)(2,1)S(1)}, u32[]{:S(2)}, u32[]{:S(2)}) collective-permute-start(bf16[32,2048]{1,0:T(8,128)(2,1)} %get-tuple-element.84), channel_id=1, source_target_pairs={{0,2},{1,3},{2,0},{3,1},{4,6},{5,7},{6,4},{7,5},{8,10},{9,11},{10,... | collective-permute-start | bytes 393224 | tf_op jit(solution)/shard_map/ppermute | solution.py:406
  12.8 8.6 %collective-permute-start.6 = (bf16[32,2048]{1,0:T(8,128)(2,1)}, bf16[32,2048]{1,0:T(8,128)(2,1)S(1)}, u32[]{:S(2)}, u32[]{:S(2)}) collective-permute-start(bf16[32,2048]{1,0:T(8,128)(2,1)} %get-tuple-element.85), channel_id=1, source_target_pairs={{0,3},{1,2},{2,1},{3,0},{4,7},{5,6},{6,5},{7,4},{8,11},{9,10},{10,... | collective-permute-start | bytes 393224 | tf_op jit(solution)/shard_map/ppermute | solution.py:406
  13.7 20.2 %collective-permute-start.23 = (bf16[80,2048]{1,0:T(8,128)(2,1)}, bf16[80,2048]{1,0:T(8,128)(2,1)S(1)}, u32[]{:S(2)}, u32[]{:S(2)}) collective-permute-start(bf16[80,2048]{1,0:T(8,128)(2,1)} %get-tuple-element.107), channel_id=1, source_target_pairs={{0,8},{4,12},{8,24},{12,28},{16,0},{20,4},{24,16},{28,20},{1,9},{5... | collective-permute-start | bytes 983048 | tf_op jit(solution)/shard_map/ppermute | solution.py:404
  15.9 27.2 %collective-permute-start.27 = (bf16[80,2048]{1,0:T(8,128)(2,1)}, bf16[80,2048]{1,0:T(8,128)(2,1)S(1)}, u32[]{:S(2)}, u32[]{:S(2)}) collective-permute-start(bf16[80,2048]{1,0:T(8,128)(2,1)} %get-tuple-element.112), channel_id=1, source_target_pairs={{0,16},{4,20},{8,0},{12,4},{16,24},{20,28},{24,8},{28,12},{1,17},{... | collective-permute-start | bytes 983048 | tf_op jit(solution)/shard_map/ppermute | solution.py:404
  19.3 5.9 %collective-permute-start.7 = (bf16[32,2048]{1,0:T(8,128)(2,1)}, bf16[32,2048]{1,0:T(8,128)(2,1)S(1)}, u32[]{:S(2)}, u32[]{:S(2)}) collective-permute-start(bf16[32,2048]{1,0:T(8,128)(2,1)} %get-tuple-element.86), channel_id=1, source_target_pairs={{0,4},{4,0},{8,12},{12,8},{16,20},{20,16},{24,28},{28,24},{1,5},{5... | collective-permute-start | bytes 393224 | tf_op jit(solution)/shard_map/ppermute | solution.py:404
  20.8 7.0 %collective-permute-start.8 = (bf16[32,2048]{1,0:T(8,128)(2,1)}, bf16[32,2048]{1,0:T(8,128)(2,1)S(1)}, u32[]{:S(2)}, u32[]{:S(2)}) collective-permute-start(bf16[32,2048]{1,0:T(8,128)(2,1)} %get-tuple-element.87), channel_id=1, source_target_pairs={{0,5},{1,4},{2,7},{3,6},{4,1},{5,0},{6,3},{7,2},{8,13},{9,12},{10,... | collective-permute-start | bytes 393224 | tf_op jit(solution)/shard_map/ppermute | solution.py:410
  21.4 9.9 %collective-permute-start.9 = (bf16[32,2048]{1,0:T(8,128)(2,1)}, bf16[32,2048]{1,0:T(8,128)(2,1)S(1)}, u32[]{:S(2)}, u32[]{:S(2)}) collective-permute-start(bf16[32,2048]{1,0:T(8,128)(2,1)} %get-tuple-element.88), channel_id=1, source_target_pairs={{0,6},{1,7},{2,4},{3,5},{4,2},{5,3},{6,0},{7,1},{8,14},{9,15},{10,... | collective-permute-start | bytes 393224 | tf_op jit(solution)/shard_map/ppermute | solution.py:410
  25.2 53.0 %collective-permute-start.19 = (bf16[80,2048]{1,0:T(8,128)(2,1)S(1)}, bf16[80,2048]{1,0:T(8,128)(2,1)S(1)}, u32[]{:S(2)}, u32[]{:S(2)}) collective-permute-start(bf16[80,2048]{1,0:T(8,128)(2,1)S(1)} %copy-done.4), channel_id=1, source_target_pairs={{0,24},{4,28},{8,16},{12,20},{16,8},{20,12},{24,0},{28,4},{1,25},{... | collective-permute-start | bytes 983048 | tf_op jit(solution)/shard_map/ppermute | solution.py:404
  27.9 50.6 %collective-permute-start.11 = (bf16[80,2048]{1,0:T(8,128)(2,1)}, bf16[80,2048]{1,0:T(8,128)(2,1)S(1)}, u32[]{:S(2)}, u32[]{:S(2)}) collective-permute-start(bf16[80,2048]{1,0:T(8,128)(2,1)} %get-tuple-element.92), channel_id=1, source_target_pairs={{0,12},{4,8},{8,28},{12,24},{16,4},{20,0},{24,20},{28,16},{1,13},{... | collective-permute-start | bytes 983048 | tf_op jit(solution)/shard_map/ppermute | solution.py:404
  31.3 47.5 %collective-permute-start.15 = (bf16[80,2048]{1,0:T(8,128)(2,1)}, bf16[80,2048]{1,0:T(8,128)(2,1)S(1)}, u32[]{:S(2)}, u32[]{:S(2)}) collective-permute-start(bf16[80,2048]{1,0:T(8,128)(2,1)} %get-tuple-element.97), channel_id=1, source_target_pairs={{0,20},{4,16},{8,4},{12,0},{16,28},{20,24},{24,12},{28,8},{1,21},{... | collective-permute-start | bytes 983048 | tf_op jit(solution)/shard_map/ppermute | solution.py:404
  33.8 42.7 %collective-permute-start.31 = (bf16[80,1024]{1,0:T(8,128)(2,1)}, bf16[80,1024]{1,0:T(8,128)(2,1)S(1)}, u32[]{:S(2)}, u32[]{:S(2)}) collective-permute-start(bf16[80,1024]{1,0:T(8,128)(2,1)} %get-tuple-element.133), channel_id=1, source_target_pairs={{0,28},{4,24},{8,20},{12,16},{16,12},{20,8},{24,4},{28,0},{1,29},{... | collective-permute-start | bytes 491528 | tf_op jit(solution)/shard_map/ppermute | solution.py:404
  43.1 33.5 %collective-permute-start = (bf16[80,1024]{1,0:T(8,128)(2,1)}, bf16[80,1024]{1,0:T(8,128)(2,1)S(1)}, u32[]{:S(2)}, u32[]{:S(2)}) collective-permute-start(bf16[80,1024]{1,0:T(8,128)(2,1)} %get-tuple-element.75), channel_id=1, source_target_pairs={{0,28},{4,24},{8,20},{12,16},{16,12},{20,8},{24,4},{28,0},{1,29},{... | collective-permute-start | bytes 491528 | tf_op jit(solution)/shard_map/ppermute | solution.py:404
  76.5 4.5 %collective-permute-start.24 = (bf16[32,2048]{1,0:T(8,128)(2,1)S(1)}, bf16[32,2048]{1,0:T(8,128)(2,1)S(1)}, u32[]{:S(2)}, u32[]{:S(2)}) collective-permute-start(bf16[32,2048]{1,0:T(8,128)(2,1)S(1)} %get-tuple-element.109), channel_id=1, source_target_pairs={{0,1},{1,0},{2,3},{3,2},{4,5},{5,4},{6,7},{7,6},{8,9},{9,8},{10,11... | collective-permute-start | bytes 393224 | tf_op jit(solution)/shard_map/ppermute | solution.py:406
  76.6 6.4 %collective-permute-start.25 = (bf16[32,2048]{1,0:T(8,128)(2,1)S(1)}, bf16[32,2048]{1,0:T(8,128)(2,1)S(1)}, u32[]{:S(2)}, u32[]{:S(2)}) collective-permute-start(bf16[32,2048]{1,0:T(8,128)(2,1)S(1)} %get-tuple-element.110), channel_id=1, source_target_pairs={{0,2},{1,3},{2,0},{3,1},{4,6},{5,7},{6,4},{7,5},{8,10},{9,11},{10,... | collective-permute-start | bytes 393224 | tf_op jit(solution)/shard_map/ppermute | solution.py:406
  78.1 6.7 %collective-permute-start.26 = (bf16[32,2048]{1,0:T(8,128)(2,1)S(1)}, bf16[32,2048]{1,0:T(8,128)(2,1)S(1)}, u32[]{:S(2)}, u32[]{:S(2)}) collective-permute-start(bf16[32,2048]{1,0:T(8,128)(2,1)S(1)} %get-tuple-element.111), channel_id=1, source_target_pairs={{0,3},{1,2},{2,1},{3,0},{4,7},{5,6},{6,5},{7,4},{8,11},{9,10},{10,... | collective-permute-start | bytes 393224 | tf_op jit(solution)/shard_map/ppermute | solution.py:406
  78.5 7.8 %collective-permute-start.28 = (bf16[32,2048]{1,0:T(8,128)(2,1)S(1)}, bf16[32,2048]{1,0:T(8,128)(2,1)S(1)}, u32[]{:S(2)}, u32[]{:S(2)}) collective-permute-start(bf16[32,2048]{1,0:T(8,128)(2,1)S(1)} %get-tuple-element.114), channel_id=1, source_target_pairs={{0,1},{1,0},{2,3},{3,2},{4,5},{5,4},{6,7},{7,6},{8,9},{9,8},{10,11... | collective-permute-start | bytes 393224 | tf_op jit(solution)/shard_map/ppermute | solution.py:406
  78.8 9.8 %collective-permute-start.29 = (bf16[32,2048]{1,0:T(8,128)(2,1)S(1)}, bf16[32,2048]{1,0:T(8,128)(2,1)S(1)}, u32[]{:S(2)}, u32[]{:S(2)}) collective-permute-start(bf16[32,2048]{1,0:T(8,128)(2,1)S(1)} %get-tuple-element.115), channel_id=1, source_target_pairs={{0,2},{1,3},{2,0},{3,1},{4,6},{5,7},{6,4},{7,5},{8,10},{9,11},{10,... | collective-permute-start | bytes 393224 | tf_op jit(solution)/shard_map/ppermute | solution.py:406
  81.0 10.3 %collective-permute-start.30 = (bf16[32,2048]{1,0:T(8,128)(2,1)S(1)}, bf16[32,2048]{1,0:T(8,128)(2,1)S(1)}, u32[]{:S(2)}, u32[]{:S(2)}) collective-permute-start(bf16[32,2048]{1,0:T(8,128)(2,1)S(1)} %get-tuple-element.116), channel_id=1, source_target_pairs={{0,3},{1,2},{2,1},{3,0},{4,7},{5,6},{6,5},{7,4},{8,11},{9,10},{10,... | collective-permute-start | bytes 393224 | tf_op jit(solution)/shard_map/ppermute | solution.py:406
  83.1 9.8 %collective-permute-start.20 = (bf16[32,2048]{1,0:T(8,128)(2,1)S(1)}, bf16[32,2048]{1,0:T(8,128)(2,1)S(1)}, u32[]{:S(2)}, u32[]{:S(2)}) collective-permute-start(bf16[32,2048]{1,0:T(8,128)(2,1)S(1)} %get-tuple-element.104), channel_id=1, source_target_pairs={{0,1},{1,0},{2,3},{3,2},{4,5},{5,4},{6,7},{7,6},{8,9},{9,8},{10,11... | collective-permute-start | bytes 393224 | tf_op jit(solution)/shard_map/ppermute | solution.py:406
  84.8 9.5 %collective-permute-start.21 = (bf16[32,2048]{1,0:T(8,128)(2,1)S(1)}, bf16[32,2048]{1,0:T(8,128)(2,1)S(1)}, u32[]{:S(2)}, u32[]{:S(2)}) collective-permute-start(bf16[32,2048]{1,0:T(8,128)(2,1)S(1)} %get-tuple-element.105), channel_id=1, source_target_pairs={{0,2},{1,3},{2,0},{3,1},{4,6},{5,7},{6,4},{7,5},{8,10},{9,11},{10,... | collective-permute-start | bytes 393224 | tf_op jit(solution)/shard_map/ppermute | solution.py:406
  86.2 9.8 %collective-permute-start.22 = (bf16[32,2048]{1,0:T(8,128)(2,1)S(1)}, bf16[32,2048]{1,0:T(8,128)(2,1)S(1)}, u32[]{:S(2)}, u32[]{:S(2)}) collective-permute-start(bf16[32,2048]{1,0:T(8,128)(2,1)S(1)} %get-tuple-element.106), channel_id=1, source_target_pairs={{0,3},{1,2},{2,1},{3,0},{4,7},{5,6},{6,5},{7,4},{8,11},{9,10},{10,... | collective-permute-start | bytes 393224 | tf_op jit(solution)/shard_map/ppermute | solution.py:406
  88.7 8.8 %collective-permute-start.12 = (bf16[32,2048]{1,0:T(8,128)(2,1)S(1)}, bf16[32,2048]{1,0:T(8,128)(2,1)S(1)}, u32[]{:S(2)}, u32[]{:S(2)}) collective-permute-start(bf16[32,2048]{1,0:T(8,128)(2,1)S(1)} %get-tuple-element.94), channel_id=1, source_target_pairs={{0,1},{1,0},{2,3},{3,2},{4,5},{5,4},{6,7},{7,6},{8,9},{9,8},{10,11... | collective-permute-start | bytes 393224 | tf_op jit(solution)/shard_map/ppermute | solution.py:406
  91.3 10.0 %collective-permute-start.13 = (bf16[32,2048]{1,0:T(8,128)(2,1)S(1)}, bf16[32,2048]{1,0:T(8,128)(2,1)S(1)}, u32[]{:S(2)}, u32[]{:S(2)}) collective-permute-start(bf16[32,2048]{1,0:T(8,128)(2,1)S(1)} %get-tuple-element.95), channel_id=1, source_target_pairs={{0,2},{1,3},{2,0},{3,1},{4,6},{5,7},{6,4},{7,5},{8,10},{9,11},{10,... | collective-permute-start | bytes 393224 | tf_op jit(solution)/shard_map/ppermute | solution.py:406
  92.8 8.9 %collective-permute-start.14 = (bf16[32,2048]{1,0:T(8,128)(2,1)S(1)}, bf16[32,2048]{1,0:T(8,128)(2,1)S(1)}, u32[]{:S(2)}, u32[]{:S(2)}) collective-permute-start(bf16[32,2048]{1,0:T(8,128)(2,1)S(1)} %get-tuple-element.96), channel_id=1, source_target_pairs={{0,3},{1,2},{2,1},{3,0},{4,7},{5,6},{6,5},{7,4},{8,11},{9,10},{10,... | collective-permute-start | bytes 393224 | tf_op jit(solution)/shard_map/ppermute | solution.py:406
  94.3 8.8 %collective-permute-start.16 = (bf16[32,2048]{1,0:T(8,128)(2,1)S(1)}, bf16[32,2048]{1,0:T(8,128)(2,1)S(1)}, u32[]{:S(2)}, u32[]{:S(2)}) collective-permute-start(bf16[32,2048]{1,0:T(8,128)(2,1)S(1)} %get-tuple-element.99), channel_id=1, source_target_pairs={{0,1},{1,0},{2,3},{3,2},{4,5},{5,4},{6,7},{7,6},{8,9},{9,8},{10,11... | collective-permute-start | bytes 393224 | tf_op jit(solution)/shard_map/ppermute | solution.py:406
  96.1 9.5 %collective-permute-start.17 = (bf16[32,2048]{1,0:T(8,128)(2,1)S(1)}, bf16[32,2048]{1,0:T(8,128)(2,1)S(1)}, u32[]{:S(2)}, u32[]{:S(2)}) collective-permute-start(bf16[32,2048]{1,0:T(8,128)(2,1)S(1)} %get-tuple-element.100), channel_id=1, source_target_pairs={{0,2},{1,3},{2,0},{3,1},{4,6},{5,7},{6,4},{7,5},{8,10},{9,11},{10,... | collective-permute-start | bytes 393224 | tf_op jit(solution)/shard_map/ppermute | solution.py:406
  97.5 9.8 %collective-permute-start.18 = (bf16[32,2048]{1,0:T(8,128)(2,1)S(1)}, bf16[32,2048]{1,0:T(8,128)(2,1)S(1)}, u32[]{:S(2)}, u32[]{:S(2)}) collective-permute-start(bf16[32,2048]{1,0:T(8,128)(2,1)S(1)} %get-tuple-element.101), channel_id=1, source_target_pairs={{0,3},{1,2},{2,1},{3,0},{4,7},{5,6},{6,5},{7,4},{8,11},{9,10},{10,... | collective-permute-start | bytes 393224 | tf_op jit(solution)/shard_map/ppermute | solution.py:406
  101.4 9.6 %collective-permute-start.32 = (bf16[32,1024]{1,0:T(8,128)(2,1)S(1)}, bf16[32,1024]{1,0:T(8,128)(2,1)S(1)}, u32[]{:S(2)}, u32[]{:S(2)}) collective-permute-start(bf16[32,1024]{1,0:T(8,128)(2,1)S(1)} %get-tuple-element.135), channel_id=1, source_target_pairs={{0,1},{1,0},{2,3},{3,2},{4,5},{5,4},{6,7},{7,6},{8,9},{9,8},{10,11... | collective-permute-start | bytes 196616 | tf_op jit(solution)/shard_map/ppermute | solution.py:406
  101.7 10.1 %collective-permute-start.33 = (bf16[32,1024]{1,0:T(8,128)(2,1)S(1)}, bf16[32,1024]{1,0:T(8,128)(2,1)S(1)}, u32[]{:S(2)}, u32[]{:S(2)}) collective-permute-start(bf16[32,1024]{1,0:T(8,128)(2,1)S(1)} %get-tuple-element.136), channel_id=1, source_target_pairs={{0,2},{1,3},{2,0},{3,1},{4,6},{5,7},{6,4},{7,5},{8,10},{9,11},{10,... | collective-permute-start | bytes 196616 | tf_op jit(solution)/shard_map/ppermute | solution.py:406
  103.1 8.7 %collective-permute-start.34 = (bf16[32,1024]{1,0:T(8,128)(2,1)S(1)}, bf16[32,1024]{1,0:T(8,128)(2,1)S(1)}, u32[]{:S(2)}, u32[]{:S(2)}) collective-permute-start(bf16[32,1024]{1,0:T(8,128)(2,1)S(1)} %get-tuple-element.137), channel_id=1, source_target_pairs={{0,3},{1,2},{2,1},{3,0},{4,7},{5,6},{6,5},{7,4},{8,11},{9,10},{10,... | collective-permute-start | bytes 196616 | tf_op jit(solution)/shard_map/ppermute | solution.py:406
  105.5 7.2 %collective-permute-start.1 = (bf16[32,1024]{1,0:T(8,128)(2,1)S(1)}, bf16[32,1024]{1,0:T(8,128)(2,1)S(1)}, u32[]{:S(2)}, u32[]{:S(2)}) collective-permute-start(bf16[32,1024]{1,0:T(8,128)(2,1)S(1)} %get-tuple-element.77), channel_id=1, source_target_pairs={{0,1},{1,0},{2,3},{3,2},{4,5},{5,4},{6,7},{7,6},{8,9},{9,8},{10,11... | collective-permute-start | bytes 196616 | tf_op jit(solution)/shard_map/ppermute | solution.py:406
  107.3 5.4 %collective-permute-start.2 = (bf16[32,1024]{1,0:T(8,128)(2,1)S(1)}, bf16[32,1024]{1,0:T(8,128)(2,1)S(1)}, u32[]{:S(2)}, u32[]{:S(2)}) collective-permute-start(bf16[32,1024]{1,0:T(8,128)(2,1)S(1)} %get-tuple-element.78), channel_id=1, source_target_pairs={{0,2},{1,3},{2,0},{3,1},{4,6},{5,7},{6,4},{7,5},{8,10},{9,11},{10,... | collective-permute-start | bytes 196616 | tf_op jit(solution)/shard_map/ppermute | solution.py:406
  110.9 3.8 %collective-permute-start.3 = (bf16[32,1024]{1,0:T(8,128)(2,1)S(1)}, bf16[32,1024]{1,0:T(8,128)(2,1)S(1)}, u32[]{:S(2)}, u32[]{:S(2)}) collective-permute-start(bf16[32,1024]{1,0:T(8,128)(2,1)S(1)} %get-tuple-element.79), channel_id=1, source_target_pairs={{0,3},{1,2},{2,1},{3,0},{4,7},{5,6},{6,5},{7,4},{8,11},{9,10},{10,... | collective-permute-start | bytes 196616 | tf_op jit(solution)/shard_map/ppermute | solution.py:406
  114.7 12.8 %copy-start.2 = (s32[8,512]{1,0:T(8,128)S(1)}, s32[8,512]{1,0:T(8,128)}, u32[]{:S(2)}) copy-start(s32[8,512]{1,0:T(8,128)} %get-tuple-element.74.key_hbm.key_ref) | copy-start | bytes 49156

commit v2 on v1

--- a/solution.py
+++ b/solution.py
@@ -113,7 +113,7 @@
     root = math.sqrt(width)
     far, direct, relayed, stages = plan()
     source = lambda m, e: back_shift(lax.axis_index("dp"), m) * cent + (lax.axis_index("cent") ^ e)
-    span = lambda f: (f[1] * width // 4, f[2] * width // 4)
+    span = lambda f: (f[1] * width // 8, f[2] * width // 8)
     size = lambda f: span(f)[1] - span(f)[0]
 
     def route(assigned_hbm, table_hbm, docs_hbm, far_ref, tag_ref, key_ref, *scratch):
@@ -193,10 +193,11 @@
         key, row_key = key_ref[0:1, :], key_ref[1:2, :]
         rest = sorted({f[0] for f in far[1:]})
         sel = [iota((row_cap, docs), 0) + m * row_cap == row_key for m in rest]
-        sel += [iota((group, docs), 0) + m * group == key for m in direct]
+        ahead = stages[-1][-1][0]
+        sel += [iota((group, docs), 0) + m * group == key for m in direct + [ahead[0]]]
         sel = jnp.concatenate([v.astype(jnp.bfloat16) for v in sel], axis=0)
         copies[1].wait()
-        step = width // 4
+        step = width // 8
         for lo in range(0, width, step):
             picked = mm(sel, docs_ref[:, lo : lo + step], ((1,), (0,))).astype(jnp.bfloat16)
             for ref, f in zip(outs, far[1:]):
@@ -206,7 +207,15 @@
                     ref[:, lane : lane + step] = picked[at : at + row_cap]
             for n, ref in enumerate(outs[len(far) - 1 :]):
                 at = len(rest) * row_cap + n * cap
-                ref[:, lo : lo + step] = picked[at : at + cap]
+                if n < len(direct) * cent:
+                    ref[:, lo : lo + step] = picked[at : at + cap]
+                elif span(ahead)[0] <= lo < span(ahead)[1]:
+                    lane = lo - span(ahead)[0]
+                    ref[:, lane : lane + step] = picked[at : at + cap]
+
+    def join(*refs):
+        for n, ref in enumerate(refs[:-1]):
+            refs[-1][n * cap : (n + 1) * cap, :] = ref[...]
 
     def norms(cent_ref, keep_ref, inv_ref):
         keep_ref[...] = cent_ref[...]
@@ -255,17 +264,18 @@
         def body(*refs):
             refs = list(refs)
             take = lambda n: [refs.pop(0) for _ in range(n)]
-            arrays = [take(cent) for _ in (parts[-1:] if last else parts)]
+            arrays = [take(1)] if last else [take(cent) for _ in parts]
             tag_ref, cent_ref, cent_inv_ref = take(3)
             olds = [take(4) for _ in range(s)]
             tally = take(1)[0] if s else None
             acc_ref = take(1)[0] if last else None
             if last:
-                score_ref, stat_ref, x = take(3)
+                score_ref, stat_ref = take(2)
             else:
                 x, col, line, own_ref, tally_out = take(5)
                 old_outs = take(s)
-            fill(x, parts[-1:] if last else parts, masks, arrays)
+            if not last:
+                fill(x, parts, masks, arrays)
             lane = slice(*span(parts[-1][0])) if last else slice(None)
             base = [0]
 
@@ -301,7 +311,7 @@
                 counts = [jnp.zeros((rows, 1), jnp.float32)] * 3
             else:
                 counts = [tally[:, i : i + 1] for i in range(3)]
-            xn = x[...]
+            xn = arrays[0][0][...] if last else x[...]
             cross = dots(cent_ref, xn)
             grams = [dots(old[0], xn) for old in olds]
             own_gram = mm(xn, xn, ((1,), (1,))) + (acc_ref[base[0] :, :] if last else 0.0)
@@ -433,7 +443,8 @@
         pack,
         (key, documents),
         [bf16(row_cap, size(f)) for f in far[1:]]
-        + [bf16(cap, width)] * (len(direct) * cent),
+        + [bf16(cap, width)] * (len(direct) * cent)
+        + [bf16(cap, size(stages[-1][-1][0]))] * cent,
         2 * len(far) * row_cap * docs * width,
         [pltpu.VMEM((8, docs), jnp.int32), held, pltpu.SemaphoreType.DMA((2,))],
         mib=62,
@@ -443,7 +454,7 @@
     arrays = {}
     for n, m in enumerate(direct):
         near = got[len(far) - 1 + n * cent : len(far) - 1 + (n + 1) * cent]
-        arrays[((m, 0, 4),)] = [send(v, m, e) for e, v in enumerate(near)]
+        arrays[((m, 0, 8),)] = [send(v, m, e) for e, v in enumerate(near)]
     for part in relayed:
         wide = size(part[0])
         hop = call(
@@ -454,6 +465,11 @@
         )
         arrays[part] = [send(hop[e], 0, e) for e in range(cent)]
     kept, cent_inv = call(norms, (centroids,), [bf16(rows, width), f32(rows, 1)], 2 * rows * width)
+    ahead = stages[-1][-1][0]
+    early = got[len(far) - 1 + len(direct) * cent :]
+    early = [send(v, 0, e) for e, v in enumerate(early)]
+    (joined,) = call(join, early, [bf16(group, size(ahead))], 1 << 10)
+    arrays[(ahead,)] = [send(joined, ahead[0], 0)]
     olds, tally = [], None
     for s, parts in enumerate(stages):
         fresh = len(stage_masks(parts)) * group
@@ -474,9 +490,8 @@
             (acc,) = call(
                 partial, early, [f32(many, fresh)], flops, [pltpu.VMEM((fresh, wide), jnp.bfloat16)]
             )
-            scratch = [pltpu.VMEM((fresh, width - wide), jnp.bfloat16)]
             outs = [f32(owners, 1, 2 * cap), f32(3, rows)]
-            scores, stats = call(make_owner(s), ins + [acc], outs, flops // 4, scratch)
+            scores, stats = call(make_owner(s), ins + [acc], outs, flops // 4)
     back = exchange(scores)
     outs = [f32(1, docs), f32(1, docs), f32(3, rows)]
     proto, red, stats = call(unpack, (back, key, stats), outs, 1 << 20)
@@ -491,9 +506,9 @@
 
 
 def plan():
-    whole = lambda *masks: tuple((m, 0, 4) for m in masks)
-    cuts = [(5, 0, 2), (5, 2, 4)]
-    far = [f[0] for f in map(whole, (4, 2, 6, 3, 7))] + cuts
+    whole = lambda *masks: tuple((m, 0, 8) for m in masks)
+    cuts = [(5, 0, 5), (5, 5, 8)]
+    far = [f[0] for f in map(whole, (4, 2, 6, 3, 7))] + cuts[:1]
     relayed = [(f,) for f in far]
     direct = [0, 1]
     stages = [

time: 129 us -> 132 us (1.023)
  starting transfers between devices: 43.1 us -> 50 us
  blocking collectives: 43.7 us -> 36.9 us
  waiting for transfers between devices: 20.3 us -> 23.5 us
    ppermute x8, starting transfers between devices: 20.9 us -> 28.7 us  [send(): return lax.ppermute(value, 'dp', [(i, shift(i, m)) for i in range(dp)])]
    all_to_all x2, blocking collectives: 43.7 us -> 36.9 us  [exchange(): return lax.all_to_all(value, ('dp', 'cent'), 0, 0, tiled=True)]
    ppermute x24, waiting for transfers between devices: 14.4 us -> 20.9 us  [send(): return lax.ppermute(value, 'cent', [(j, j ^ e) for j in range(cent)])]
    ppermute x3, waiting for transfers between devices: 4.18 us -> 0.01 us  [send(): return lax.ppermute(value, ('dp', 'cent'), pairs)]
    ppermute x3, starting transfers between devices: 5.48 us -> 3.44 us  [send(): return lax.ppermute(value, ('dp', 'cent'), pairs)]
  transfers between devices with their start and end apart: 35 -> 35, of which waited for: 14 -> 10; matrix products, arithmetic and copies ran while one was open for 0% -> 0% of each run, Pallas kernels for 8% -> 8%
where the time goes in v2:
time: 132 us
  starting transfers between devices  50 us (38%)
  blocking collectives  36.9 us (28%)
  waiting for transfers between devices  23.5 us (18%)
  Pallas kernels  20.6 us (16%)
    all_to_all x2, blocking collectives, exchange(): return lax.all_to_all(value, ('dp', 'cent'), 0, 0, tiled=True)  36.9 us
    ppermute x8, starting transfers between devices, send(): return lax.ppermute(value, 'dp', [(i, shift(i, m)) for i in range(dp)])  28.7 us
    ppermute x24, waiting for transfers between devices, send(): return lax.ppermute(value, 'cent', [(j, j ^ e) for j in range(cent)])  20.9 us
    pallas_call x16, Pallas kernels, call(): pl.pallas_call(body, out_shape=outs, in_specs=[pl.BlockSpec(memory_space=...  20.6 us
    ppermute x24, starting transfers between devices, send(): return lax.ppermute(value, 'cent', [(j, j ^ e) for j in range(cent)])  17.9 us
    ppermute x3, starting transfers between devices, send(): return lax.ppermute(value, ('dp', 'cent'), pairs)  3.44 us
  transfers between devices with their start and end apart: 35, of which 10 were waited for; matrix products, arithmetic and copies ran while one was open for 0% of the time, Pallas kernels for 8%

profile of v2, /device:TPU:0, one launch (start us, length us, event | category | flops | bytes accessed | tf_op | source)
XLA Modules:
  0.0 132.0 jit_solution(17825846570646611457)
XLA Ops:
  0.6 2.9 %shard_map.67 = (bf16[80,2048]{1,0:T(8,128)(2,1)}, s32[32,1,128]{2,1,0:T(1,128)}, s32[8,512]{1,0:T(8,128)}) custom-call(s32[1,512]{1,0:T(1,128)} %bitcast.5, s32[96,128]{1,0:T(8,128)} %bitcast.4, bf16[512,2048]{1,0:T(8,128)(2,1)} %docs_hbm.3), custom_call_target="tpu_custom_call" | custom-call | flops 167772160 | bytes 1048576 | tf_op jit(solution)/shard_map/pallas_call | solution.py:400
  3.5 5.0 %shard_map.68 = (bf16[80,2048]{1,0:T(8,128)(2,1)}, bf16[80,2048]{1,0:T(8,128)(2,1)}, bf16[80,2048]{1,0:T(8,128)(2,1)}, bf16[80,2048]{1,0:T(8,128)(2,1)}, bf16[80...) custom-call(s32[8,512]{1,0:T(8,128)} %get-tuple-element.72.key_hbm.k, ...), custom_call_target="tpu_custom_call" | custom-call | flops 1006632960 | bytes 1048576 | tf_op jit(solution)/shard_map/pallas_call | solution.py:400
  8.6 0.6 collective-permute-start
  9.1 2.6 %collective-permute-start.1 = (bf16[32,768]{1,0:T(8,128)(2,1)}, bf16[32,768]{1,0:T(8,128)(2,1)S(1)}, u32[]{:S(2)}, u32[]{:S(2)}) collective-permute-start(bf16[32,768]{1,0:T(8,128)(2,1)} %get-tuple-element.75), channel_id=1, source_target_pairs={{0,2},{1,3},{2,0},{3,1},{4,6},{5,7},{6,4},{7,5},{8,10},{9,11},{10,... | collective-permute-start | bytes 147464 | tf_op jit(solution)/shard_map/ppermute | solution.py:416
  11.7 1.2 collective-permute-start.10
  12.9 0.4 collective-permute-start.4
  13.2 1.5 %collective-permute-start.5 = (bf16[32,2048]{1,0:T(8,128)(2,1)}, bf16[32,2048]{1,0:T(8,128)(2,1)S(1)}, u32[]{:S(2)}, u32[]{:S(2)}) collective-permute-start(bf16[32,2048]{1,0:T(8,128)(2,1)} %get-tuple-element.82), channel_id=1, source_target_pairs={{0,2},{1,3},{2,0},{3,1},{4,6},{5,7},{6,4},{7,5},{8,10},{9,11},{10,... | collective-permute-start | bytes 393224 | tf_op jit(solution)/shard_map/ppermute | solution.py:416
  14.8 1.7 %collective-permute-start.2 = (bf16[32,768]{1,0:T(8,128)(2,1)}, bf16[32,768]{1,0:T(8,128)(2,1)S(1)}, u32[]{:S(2)}, u32[]{:S(2)}) collective-permute-start(bf16[32,768]{1,0:T(8,128)(2,1)} %get-tuple-element.76), channel_id=1, source_target_pairs={{0,3},{1,2},{2,1},{3,0},{4,7},{5,6},{6,5},{7,4},{8,11},{9,10},{10,... | collective-permute-start | bytes 147464 | tf_op jit(solution)/shard_map/ppermute | solution.py:416
  16.5 8.7 %collective-permute-done.2.refs_3_ = bf16[32,768]{1,0:T(8,128)(2,1)S(1)} collective-permute-done((bf16[32,768]{1,0:T(8,128)(2,1)}, bf16[32,768]{1,0:T(8,128)(2,1)S(1)}, u32[]{:S(2)}, u32[]{:S(2)}) %collective-permute-start.2) | collective-permute-done | bytes 49184 | tf_op jit(solution)/shard_map/ppermute | solution.py:416
  25.2 1.6 %collective-permute-start.23 = (bf16[80,2048]{1,0:T(8,128)(2,1)}, bf16[80,2048]{1,0:T(8,128)(2,1)S(1)}, u32[]{:S(2)}, u32[]{:S(2)}) collective-permute-start(bf16[80,2048]{1,0:T(8,128)(2,1)} %get-tuple-element.105), channel_id=1, source_target_pairs={{0,8},{4,12},{8,24},{12,28},{16,0},{20,4},{24,16},{28,20},{1,9},{5... | collective-permute-start | bytes 983048 | tf_op jit(solution)/shard_map/ppermute | solution.py:414
  26.8 0.4 collective-permute-start.7
  27.1 0.8 collective-permute-start.8
  28.0 1.4 %collective-permute-start.9 = (bf16[32,2048]{1,0:T(8,128)(2,1)}, bf16[32,2048]{1,0:T(8,128)(2,1)S(1)}, u32[]{:S(2)}, u32[]{:S(2)}) collective-permute-start(bf16[32,2048]{1,0:T(8,128)(2,1)} %get-tuple-element.86), channel_id=1, source_target_pairs={{0,6},{1,7},{2,4},{3,5},{4,2},{5,3},{6,0},{7,1},{8,14},{9,15},{10,... | collective-permute-start | bytes 393224 | tf_op jit(solution)/shard_map/ppermute | solution.py:420
  29.4 1.3 %collective-permute-start.27 = (bf16[80,2048]{1,0:T(8,128)(2,1)}, bf16[80,2048]{1,0:T(8,128)(2,1)S(1)}, u32[]{:S(2)}, u32[]{:S(2)}) collective-permute-start(bf16[80,2048]{1,0:T(8,128)(2,1)} %get-tuple-element.110), channel_id=1, source_target_pairs={{0,16},{4,20},{8,0},{12,4},{16,24},{20,28},{24,8},{28,12},{1,17},{... | collective-permute-start | bytes 983048 | tf_op jit(solution)/shard_map/ppermute | solution.py:414
  30.8 2.6 %collective-permute-done.7.refs_4_ = bf16[32,2048]{1,0:T(8,128)(2,1)S(1)} collective-permute-done((bf16[32,2048]{1,0:T(8,128)(2,1)}, bf16[32,2048]{1,0:T(8,128)(2,1)S(1)}, u32[]{:S(2)}, u32[]{:S(2)}) %collective-permute-start.7) | collective-permute-done | bytes 131104 | tf_op jit(solution)/shard_map/ppermute | solution.py:414
  33.4 2.5 %collective-permute-start.19 = (bf16[80,2048]{1,0:T(8,128)(2,1)S(1)}, bf16[80,2048]{1,0:T(8,128)(2,1)S(1)}, u32[]{:S(2)}, u32[]{:S(2)}) collective-permute-start(bf16[80,2048]{1,0:T(8,128)(2,1)S(1)} %copy-done.5), channel_id=1, source_target_pairs={{0,24},{4,28},{8,16},{12,20},{16,8},{20,12},{24,0},{28,4},{1,25},{... | collective-permute-start | bytes 983048 | tf_op jit(solution)/shard_map/ppermute | solution.py:414
  35.8 2.0 %collective-permute-start.11 = (bf16[80,2048]{1,0:T(8,128)(2,1)}, bf16[80,2048]{1,0:T(8,128)(2,1)S(1)}, u32[]{:S(2)}, u32[]{:S(2)}) collective-permute-start(bf16[80,2048]{1,0:T(8,128)(2,1)} %get-tuple-element.90), channel_id=1, source_target_pairs={{0,12},{4,8},{8,28},{12,24},{16,4},{20,0},{24,20},{28,16},{1,13},{... | collective-permute-start | bytes 983048 | tf_op jit(solution)/shard_map/ppermute | solution.py:414
  37.8 2.2 %collective-permute-start.15 = (bf16[80,2048]{1,0:T(8,128)(2,1)}, bf16[80,2048]{1,0:T(8,128)(2,1)S(1)}, u32[]{:S(2)}, u32[]{:S(2)}) collective-permute-start(bf16[80,2048]{1,0:T(8,128)(2,1)} %get-tuple-element.95), channel_id=1, source_target_pairs={{0,20},{4,16},{8,4},{12,0},{16,28},{20,24},{24,12},{28,8},{1,21},{... | collective-permute-start | bytes 983048 | tf_op jit(solution)/shard_map/ppermute | solution.py:414
  40.1 14.4 %collective-permute-start.31 = (bf16[80,1280]{1,0:T(8,128)(2,1)}, bf16[80,1280]{1,0:T(8,128)(2,1)S(1)}, u32[]{:S(2)}, u32[]{:S(2)}) collective-permute-start(bf16[80,1280]{1,0:T(8,128)(2,1)} %get-tuple-element.131), channel_id=1, source_target_pairs={{0,28},{4,24},{8,20},{12,16},{16,12},{20,8},{24,4},{28,0},{1,29},{... | collective-permute-start | bytes 614408 | tf_op jit(solution)/shard_map/ppermute | solution.py:414
  54.4 26.7 %all_to_all.10.refs_8_.tag_ref.refs_12_.refs_1_ = s32[32,1,128]{2,1,0:T(1,128)S(1)} all-to-all(s32[32,1,128]{2,1,0:T(1,128)S(1)} %copy-done.4), channel_id=1, replica_groups=mesh['dp'=8,'cent'=4] {'dp','cent'}, dimensions={0} | all-to-all | bytes 32768 | tf_op jit(solution)/shard_map/all_to_all | solution.py:423
  82.0 0.9 collective-permute-start.25
  82.9 1.0 collective-permute-start.26
  84.2 0.8 collective-permute-start.29
  85.0 0.8 collective-permute-start.30
  86.1 0.3 shard_map.72
  86.5 1.9 %collective-permute-done.25.refs_6_ = bf16[32,2048]{1,0:T(8,128)(2,1)S(1)} collective-permute-done((bf16[32,2048]{1,0:T(8,128)(2,1)S(1)}, bf16[32,2048]{1,0:T(8,128)(2,1)S(1)}, u32[]{:S(2)}, u32[]{:S(2)}) %collective-permute-start.25) | collective-permute-done | bytes 131104 | tf_op jit(solution)/shard_map/ppermute | solution.py:416
  88.4 1.9 %collective-permute-done.26.refs_7_ = bf16[32,2048]{1,0:T(8,128)(2,1)S(1)} collective-permute-done((bf16[32,2048]{1,0:T(8,128)(2,1)S(1)}, bf16[32,2048]{1,0:T(8,128)(2,1)S(1)}, u32[]{:S(2)}, u32[]{:S(2)}) %collective-permute-start.26) | collective-permute-done | bytes 131104 | tf_op jit(solution)/shard_map/ppermute | solution.py:416
  90.3 0.8 collective-permute-start.21
  91.1 1.3 collective-permute-start.22
  92.4 1.6 %collective-permute-done.29.refs_10_ = bf16[32,2048]{1,0:T(8,128)(2,1)S(1)} collective-permute-done((bf16[32,2048]{1,0:T(8,128)(2,1)S(1)}, bf16[32,2048]{1,0:T(8,128)(2,1)S(1)}, u32[]{:S(2)}, u32[]{:S(2)}) %collective-permute-start.29) | collective-permute-done | bytes 131104 | tf_op jit(solution)/shard_map/ppermute | solution.py:416
  94.0 1.9 %collective-permute-done.30.refs_11_ = bf16[32,2048]{1,0:T(8,128)(2,1)S(1)} collective-permute-done((bf16[32,2048]{1,0:T(8,128)(2,1)S(1)}, bf16[32,2048]{1,0:T(8,128)(2,1)S(1)}, u32[]{:S(2)}, u32[]{:S(2)}) %collective-permute-start.30) | collective-permute-done | bytes 131104 | tf_op jit(solution)/shard_map/ppermute | solution.py:416
  95.9 0.8 collective-permute-start.13
  96.7 0.4 shard_map.70
  97.2 1.3 shard_map.71
  99.1 4.3 %collective-permute-start.3 = (bf16[128,768]{1,0:T(8,128)(2,1)S(1)}, bf16[128,768]{1,0:T(8,128)(2,1)S(1)}, u32[]{:S(2)}, u32[]{:S(2)}) collective-permute-start(bf16[128,768]{1,0:T(8,128)(2,1)S(1)} %shard_map.69), channel_id=1, source_target_pairs={{0,28},{4,24},{8,20},{12,16},{16,12},{20,8},{24,4},{28,0},{1,29},{... | collective-permute-start | bytes 589832 | tf_op jit(solution)/shard_map/ppermute | solution.py:414
  103.4 0.4 collective-permute-start.14
  104.2 1.4 %collective-permute-start.17 = (bf16[32,2048]{1,0:T(8,128)(2,1)S(1)}, bf16[32,2048]{1,0:T(8,128)(2,1)S(1)}, u32[]{:S(2)}, u32[]{:S(2)}) collective-permute-start(bf16[32,2048]{1,0:T(8,128)(2,1)S(1)} %get-tuple-element.98), channel_id=1, source_target_pairs={{0,2},{1,3},{2,0},{3,1},{4,6},{5,7},{6,4},{7,5},{8,10},{9,11},{10,... | collective-permute-start | bytes 393224 | tf_op jit(solution)/shard_map/ppermute | solution.py:416
  105.7 3.1 %shard_map.77 = (bf16[384,2048]{1,0:T(8,128)(2,1)S(1)}, f32[384,2]{1,0:T(8,128)S(1)}, f32[4,384]{1,0:T(4,128)S(1)}, bf16[384,384]{1,0:T(8,128)(2,1)S(1)}, f32[384,3]{1,0:T(8,128)S(1)}, /*index=5*/f32[4,256]{1,0:T(4,128)S(1)}) custom-call(bf16[32,2048]{1,0:T(8,128)(2,1)S(1)} %get-tuple-element.101.refs_0_, ...), custom_call_target="tpu_custom_call" | custom-call | flops 1610612736 | bytes 1048576 | tf_op jit(solution)/shard_map/pallas_call | solution.py:400
  108.8 0.6 collective-permute-start.32
  109.5 1.4 %collective-permute-start.33 = (bf16[32,1280]{1,0:T(8,128)(2,1)S(1)}, bf16[32,1280]{1,0:T(8,128)(2,1)S(1)}, u32[]{:S(2)}, u32[]{:S(2)}) collective-permute-start(bf16[32,1280]{1,0:T(8,128)(2,1)S(1)} %get-tuple-element.134), channel_id=1, source_target_pairs={{0,2},{1,3},{2,0},{3,1},{4,6},{5,7},{6,4},{7,5},{8,10},{9,11},{10,... | collective-permute-start | bytes 245768 | tf_op jit(solution)/shard_map/ppermute | solution.py:416
  110.9 1.6 %collective-permute-done.17.refs_6_ = bf16[32,2048]{1,0:T(8,128)(2,1)S(1)} collective-permute-done((bf16[32,2048]{1,0:T(8,128)(2,1)S(1)}, bf16[32,2048]{1,0:T(8,128)(2,1)S(1)}, u32[]{:S(2)}, u32[]{:S(2)}) %collective-permute-start.17) | collective-permute-done | bytes 131104 | tf_op jit(solution)/shard_map/ppermute | solution.py:416
  112.5 2.0 %collective-permute-done.18.refs_7_ = bf16[32,2048]{1,0:T(8,128)(2,1)S(1)} collective-permute-done((bf16[32,2048]{1,0:T(8,128)(2,1)S(1)}, bf16[32,2048]{1,0:T(8,128)(2,1)S(1)}, u32[]{:S(2)}, u32[]{:S(2)}) %collective-permute-start.18) | collective-permute-done | bytes 131104 | tf_op jit(solution)/shard_map/ppermute | solution.py:416
  114.4 2.2 %shard_map.78 = (bf16[256,2048]{1,0:T(8,128)(2,1)S(1)}, f32[256,2]{1,0:T(8,128)S(1)}, f32[4,256]{1,0:T(4,128)S(1)}, bf16[384,256]{1,0:T(8,128)(2,1)S(1)}, f32[38...) custom-call(bf16[32,2048]{1,0:T(8,128)(2,1)S(1)} %get-tuple-element.91.refs_0_, ...), custom_call_target="tpu_custom_call" | custom-call | flops 1342177280 | bytes 1048576 | tf_op jit(solution)/shard_map/pallas_call | solution.py:400
  117.0 0.9 collective-permute-done.34.refs_3_
  118.0 1.1 shard_map.80.refs_17_
  119.1 1.7 %shard_map.81 = (f32[32,1,64]{2,1,0:T(1,128)S(1)}, f32[3,384]{1,0:T(4,128)S(1)}) custom-call(bf16[128,768]{1,0:T(8,128)(2,1)S(1)} %collective-permute-done.3.refs_0_, s32[32,1,128]{2,1,0:T(1,128)S(1)} %all_to_all.10.refs_8_.tag_ref.refs_12_.refs_1_, bf16[384,2048]{1,0:T(8,128)(2,1)S(1)} %get-tuple-element.78.refs_9_.refs_13_.refs_4_.refs_2_, ...), custom_call_target="tpu_custom_call" | custom-call | flops 184549376 | bytes 1048576 | tf_op jit(solution)/shard_map/pallas_call | solution.py:400
  120.8 10.2 %all_to_all.11.score_ref = f32[32,1,64]{2,1,0:T(1,128)S(1)} all-to-all(f32[32,1,64]{2,1,0:T(1,128)S(1)} %get-tuple-element.136), channel_id=1, replica_groups=mesh['dp'=8,'cent'=4] {'dp','cent'}, dimensions={0} | all-to-all | bytes 16384 | tf_op jit(solution)/shard_map/all_to_all | solution.py:423
  131.0 0.9 shard_map.82
  (52 shorter events, 3.0 us)
Async XLA Ops:
  3.5 29.8 %copy-start.5 = (bf16[80,2048]{1,0:T(8,128)(2,1)S(1)}, bf16[80,2048]{1,0:T(8,128)(2,1)}, u32[]{:S(2)}) copy-start(bf16[80,2048]{1,0:T(8,128)(2,1)} %get-tuple-element.100) | copy-start | bytes 983044
  3.5 50.9 %copy-start.4 = (s32[32,1,128]{2,1,0:T(1,128)S(1)}, s32[32,1,128]{2,1,0:T(1,128)}, u32[]{:S(2)}) copy-start(s32[32,1,128]{2,1,0:T(1,128)} %get-tuple-element.77) | copy-start | bytes 49156
  3.5 93.2 %copy-start = (bf16[384,2048]{1,0:T(8,128)(2,1)S(1)}, bf16[384,2048]{1,0:T(8,128)(2,1)}, u32[]{:S(2)}) copy-start(bf16[384,2048]{1,0:T(8,128)(2,1)} %cent_ref.1) | copy-start | bytes 4718596
  8.5 88.6 %copy-start.2 = (bf16[32,768]{1,0:T(8,128)(2,1)S(1)}, bf16[32,768]{1,0:T(8,128)(2,1)}, u32[]{:S(2)}) copy-start(bf16[32,768]{1,0:T(8,128)(2,1)} %get-tuple-element.73.refs_0_) | copy-start | bytes 147460
  8.6 6.2 %collective-permute-start = (bf16[32,768]{1,0:T(8,128)(2,1)}, bf16[32,768]{1,0:T(8,128)(2,1)S(1)}, u32[]{:S(2)}, u32[]{:S(2)}) collective-permute-start(bf16[32,768]{1,0:T(8,128)(2,1)} %get-tuple-element.74), channel_id=1, source_target_pairs={{0,1},{1,0},{2,3},{3,2},{4,5},{5,4},{6,7},{7,6},{8,9},{9,8},{10,11... | collective-permute-start | bytes 147464 | tf_op jit(solution)/shard_map/ppermute | solution.py:416
  9.1 5.7 %collective-permute-start.1 = (bf16[32,768]{1,0:T(8,128)(2,1)}, bf16[32,768]{1,0:T(8,128)(2,1)S(1)}, u32[]{:S(2)}, u32[]{:S(2)}) collective-permute-start(bf16[32,768]{1,0:T(8,128)(2,1)} %get-tuple-element.75), channel_id=1, source_target_pairs={{0,2},{1,3},{2,0},{3,1},{4,6},{5,7},{6,4},{7,5},{8,10},{9,11},{10,... | collective-permute-start | bytes 147464 | tf_op jit(solution)/shard_map/ppermute | solution.py:416
  11.7 15.1 %collective-permute-start.10 = (bf16[32,2048]{1,0:T(8,128)(2,1)}, bf16[32,2048]{1,0:T(8,128)(2,1)S(1)}, u32[]{:S(2)}, u32[]{:S(2)}) collective-permute-start(bf16[32,2048]{1,0:T(8,128)(2,1)} %get-tuple-element.87), channel_id=1, source_target_pairs={{0,7},{1,6},{2,5},{3,4},{4,3},{5,2},{6,1},{7,0},{8,15},{9,14},{10,... | collective-permute-start | bytes 393224 | tf_op jit(solution)/shard_map/ppermute | solution.py:420
  12.9 14.3 %collective-permute-start.4 = (bf16[32,2048]{1,0:T(8,128)(2,1)}, bf16[32,2048]{1,0:T(8,128)(2,1)S(1)}, u32[]{:S(2)}, u32[]{:S(2)}) collective-permute-start(bf16[32,2048]{1,0:T(8,128)(2,1)} %get-tuple-element.81), channel_id=1, source_target_pairs={{0,1},{1,0},{2,3},{3,2},{4,5},{5,4},{6,7},{7,6},{8,9},{9,8},{10,11... | collective-permute-start | bytes 393224 | tf_op jit(solution)/shard_map/ppermute | solution.py:416
  13.2 14.7 %collective-permute-start.5 = (bf16[32,2048]{1,0:T(8,128)(2,1)}, bf16[32,2048]{1,0:T(8,128)(2,1)S(1)}, u32[]{:S(2)}, u32[]{:S(2)}) collective-permute-start(bf16[32,2048]{1,0:T(8,128)(2,1)} %get-tuple-element.82), channel_id=1, source_target_pairs={{0,2},{1,3},{2,0},{3,1},{4,6},{5,7},{6,4},{7,5},{8,10},{9,11},{10,... | collective-permute-start | bytes 393224 | tf_op jit(solution)/shard_map/ppermute | solution.py:416
  14.8 14.6 %collective-permute-start.6 = (bf16[32,2048]{1,0:T(8,128)(2,1)}, bf16[32,2048]{1,0:T(8,128)(2,1)S(1)}, u32[]{:S(2)}, u32[]{:S(2)}) collective-permute-start(bf16[32,2048]{1,0:T(8,128)(2,1)} %get-tuple-element.83), channel_id=1, source_target_pairs={{0,3},{1,2},{2,1},{3,0},{4,7},{5,6},{6,5},{7,4},{8,11},{9,10},{10,... | collective-permute-start | bytes 393224 | tf_op jit(solution)/shard_map/ppermute | solution.py:416
  14.8 10.4 %collective-permute-start.2 = (bf16[32,768]{1,0:T(8,128)(2,1)}, bf16[32,768]{1,0:T(8,128)(2,1)S(1)}, u32[]{:S(2)}, u32[]{:S(2)}) collective-permute-start(bf16[32,768]{1,0:T(8,128)(2,1)} %get-tuple-element.76), channel_id=1, source_target_pairs={{0,3},{1,2},{2,1},{3,0},{4,7},{5,6},{6,5},{7,4},{8,11},{9,10},{10,... | collective-permute-start | bytes 147464 | tf_op jit(solution)/shard_map/ppermute | solution.py:416
  25.2 14.9 %collective-permute-start.23 = (bf16[80,2048]{1,0:T(8,128)(2,1)}, bf16[80,2048]{1,0:T(8,128)(2,1)S(1)}, u32[]{:S(2)}, u32[]{:S(2)}) collective-permute-start(bf16[80,2048]{1,0:T(8,128)(2,1)} %get-tuple-element.105), channel_id=1, source_target_pairs={{0,8},{4,12},{8,24},{12,28},{16,0},{20,4},{24,16},{28,20},{1,9},{5... | collective-permute-start | bytes 983048 | tf_op jit(solution)/shard_map/ppermute | solution.py:414
  26.8 6.6 %collective-permute-start.7 = (bf16[32,2048]{1,0:T(8,128)(2,1)}, bf16[32,2048]{1,0:T(8,128)(2,1)S(1)}, u32[]{:S(2)}, u32[]{:S(2)}) collective-permute-start(bf16[32,2048]{1,0:T(8,128)(2,1)} %get-tuple-element.84), channel_id=1, source_target_pairs={{0,4},{4,0},{8,12},{12,8},{16,20},{20,16},{24,28},{28,24},{1,5},{5... | collective-permute-start | bytes 393224 | tf_op jit(solution)/shard_map/ppermute | solution.py:414
  27.1 8.7 %collective-permute-start.8 = (bf16[32,2048]{1,0:T(8,128)(2,1)}, bf16[32,2048]{1,0:T(8,128)(2,1)S(1)}, u32[]{:S(2)}, u32[]{:S(2)}) collective-permute-start(bf16[32,2048]{1,0:T(8,128)(2,1)} %get-tuple-element.85), channel_id=1, source_target_pairs={{0,5},{1,4},{2,7},{3,6},{4,1},{5,0},{6,3},{7,2},{8,13},{9,12},{10,... | collective-permute-start | bytes 393224 | tf_op jit(solution)/shard_map/ppermute | solution.py:420
  28.0 9.9 %collective-permute-start.9 = (bf16[32,2048]{1,0:T(8,128)(2,1)}, bf16[32,2048]{1,0:T(8,128)(2,1)S(1)}, u32[]{:S(2)}, u32[]{:S(2)}) collective-permute-start(bf16[32,2048]{1,0:T(8,128)(2,1)} %get-tuple-element.86), channel_id=1, source_target_pairs={{0,6},{1,7},{2,4},{3,5},{4,2},{5,3},{6,0},{7,1},{8,14},{9,15},{10,... | collective-permute-start | bytes 393224 | tf_op jit(solution)/shard_map/ppermute | solution.py:420
  29.4 52.1 %collective-permute-start.27 = (bf16[80,2048]{1,0:T(8,128)(2,1)}, bf16[80,2048]{1,0:T(8,128)(2,1)S(1)}, u32[]{:S(2)}, u32[]{:S(2)}) collective-permute-start(bf16[80,2048]{1,0:T(8,128)(2,1)} %get-tuple-element.110), channel_id=1, source_target_pairs={{0,16},{4,20},{8,0},{12,4},{16,24},{20,28},{24,8},{28,12},{1,17},{... | collective-permute-start | bytes 983048 | tf_op jit(solution)/shard_map/ppermute | solution.py:414
  33.4 49.5 %collective-permute-start.19 = (bf16[80,2048]{1,0:T(8,128)(2,1)S(1)}, bf16[80,2048]{1,0:T(8,128)(2,1)S(1)}, u32[]{:S(2)}, u32[]{:S(2)}) collective-permute-start(bf16[80,2048]{1,0:T(8,128)(2,1)S(1)} %copy-done.5), channel_id=1, source_target_pairs={{0,24},{4,28},{8,16},{12,20},{16,8},{20,12},{24,0},{28,4},{1,25},{... | collective-permute-start | bytes 983048 | tf_op jit(solution)/shard_map/ppermute | solution.py:414
  35.8 48.1 %collective-permute-start.11 = (bf16[80,2048]{1,0:T(8,128)(2,1)}, bf16[80,2048]{1,0:T(8,128)(2,1)S(1)}, u32[]{:S(2)}, u32[]{:S(2)}) collective-permute-start(bf16[80,2048]{1,0:T(8,128)(2,1)} %get-tuple-element.90), channel_id=1, source_target_pairs={{0,12},{4,8},{8,28},{12,24},{16,4},{20,0},{24,20},{28,16},{1,13},{... | collective-permute-start | bytes 983048 | tf_op jit(solution)/shard_map/ppermute | solution.py:414
  37.8 46.3 %collective-permute-start.15 = (bf16[80,2048]{1,0:T(8,128)(2,1)}, bf16[80,2048]{1,0:T(8,128)(2,1)S(1)}, u32[]{:S(2)}, u32[]{:S(2)}) collective-permute-start(bf16[80,2048]{1,0:T(8,128)(2,1)} %get-tuple-element.95), channel_id=1, source_target_pairs={{0,20},{4,16},{8,4},{12,0},{16,28},{20,24},{24,12},{28,8},{1,21},{... | collective-permute-start | bytes 983048 | tf_op jit(solution)/shard_map/ppermute | solution.py:414
  40.1 41.9 %collective-permute-start.31 = (bf16[80,1280]{1,0:T(8,128)(2,1)}, bf16[80,1280]{1,0:T(8,128)(2,1)S(1)}, u32[]{:S(2)}, u32[]{:S(2)}) collective-permute-start(bf16[80,1280]{1,0:T(8,128)(2,1)} %get-tuple-element.131), channel_id=1, source_target_pairs={{0,28},{4,24},{8,20},{12,16},{16,12},{20,8},{24,4},{28,0},{1,29},{... | collective-permute-start | bytes 614408 | tf_op jit(solution)/shard_map/ppermute | solution.py:414
  81.5 15.6 %copy-start.1 = (bf16[32,2048]{1,0:T(8,128)(2,1)S(1)}, bf16[32,2048]{1,0:T(8,128)(2,1)}, u32[]{:S(2)}) copy-start(bf16[32,2048]{1,0:T(8,128)(2,1)} %get-tuple-element.80.refs_0_) | copy-start | bytes 393220
  81.5 3.5 %collective-permute-start.24 = (bf16[32,2048]{1,0:T(8,128)(2,1)S(1)}, bf16[32,2048]{1,0:T(8,128)(2,1)S(1)}, u32[]{:S(2)}, u32[]{:S(2)}) collective-permute-start(bf16[32,2048]{1,0:T(8,128)(2,1)S(1)} %get-tuple-element.107), channel_id=1, source_target_pairs={{0,1},{1,0},{2,3},{3,2},{4,5},{5,4},{6,7},{7,6},{8,9},{9,8},{10,11... | collective-permute-start | bytes 393224 | tf_op jit(solution)/shard_map/ppermute | solution.py:416
  82.0 6.4 %collective-permute-start.25 = (bf16[32,2048]{1,0:T(8,128)(2,1)S(1)}, bf16[32,2048]{1,0:T(8,128)(2,1)S(1)}, u32[]{:S(2)}, u32[]{:S(2)}) collective-permute-start(bf16[32,2048]{1,0:T(8,128)(2,1)S(1)} %get-tuple-element.108), channel_id=1, source_target_pairs={{0,2},{1,3},{2,0},{3,1},{4,6},{5,7},{6,4},{7,5},{8,10},{9,11},{10,... | collective-permute-start | bytes 393224 | tf_op jit(solution)/shard_map/ppermute | solution.py:416
  82.9 7.4 %collective-permute-start.26 = (bf16[32,2048]{1,0:T(8,128)(2,1)S(1)}, bf16[32,2048]{1,0:T(8,128)(2,1)S(1)}, u32[]{:S(2)}, u32[]{:S(2)}) collective-permute-start(bf16[32,2048]{1,0:T(8,128)(2,1)S(1)} %get-tuple-element.109), channel_id=1, source_target_pairs={{0,3},{1,2},{2,1},{3,0},{4,7},{5,6},{6,5},{7,4},{8,11},{9,10},{10,... | collective-permute-start | bytes 393224 | tf_op jit(solution)/shard_map/ppermute | solution.py:416
  83.9 7.2 %collective-permute-start.28 = (bf16[32,2048]{1,0:T(8,128)(2,1)S(1)}, bf16[32,2048]{1,0:T(8,128)(2,1)S(1)}, u32[]{:S(2)}, u32[]{:S(2)}) collective-permute-start(bf16[32,2048]{1,0:T(8,128)(2,1)S(1)} %get-tuple-element.112), channel_id=1, source_target_pairs={{0,1},{1,0},{2,3},{3,2},{4,5},{5,4},{6,7},{7,6},{8,9},{9,8},{10,11... | collective-permute-start | bytes 393224 | tf_op jit(solution)/shard_map/ppermute | solution.py:416
  84.2 9.8 %collective-permute-start.29 = (bf16[32,2048]{1,0:T(8,128)(2,1)S(1)}, bf16[32,2048]{1,0:T(8,128)(2,1)S(1)}, u32[]{:S(2)}, u32[]{:S(2)}) collective-permute-start(bf16[32,2048]{1,0:T(8,128)(2,1)S(1)} %get-tuple-element.113), channel_id=1, source_target_pairs={{0,2},{1,3},{2,0},{3,1},{4,6},{5,7},{6,4},{7,5},{8,10},{9,11},{10,... | collective-permute-start | bytes 393224 | tf_op jit(solution)/shard_map/ppermute | solution.py:416
  85.0 10.9 %collective-permute-start.30 = (bf16[32,2048]{1,0:T(8,128)(2,1)S(1)}, bf16[32,2048]{1,0:T(8,128)(2,1)S(1)}, u32[]{:S(2)}, u32[]{:S(2)}) collective-permute-start(bf16[32,2048]{1,0:T(8,128)(2,1)S(1)} %get-tuple-element.114), channel_id=1, source_target_pairs={{0,3},{1,2},{2,1},{3,0},{4,7},{5,6},{6,5},{7,4},{8,11},{9,10},{10,... | collective-permute-start | bytes 393224 | tf_op jit(solution)/shard_map/ppermute | solution.py:416
  88.4 10.7 %collective-permute-start.20 = (bf16[32,2048]{1,0:T(8,128)(2,1)S(1)}, bf16[32,2048]{1,0:T(8,128)(2,1)S(1)}, u32[]{:S(2)}, u32[]{:S(2)}) collective-permute-start(bf16[32,2048]{1,0:T(8,128)(2,1)S(1)} %get-tuple-element.102), channel_id=1, source_target_pairs={{0,1},{1,0},{2,3},{3,2},{4,5},{5,4},{6,7},{7,6},{8,9},{9,8},{10,11... | collective-permute-start | bytes 393224 | tf_op jit(solution)/shard_map/ppermute | solution.py:416
  90.3 13.2 %collective-permute-start.21 = (bf16[32,2048]{1,0:T(8,128)(2,1)S(1)}, bf16[32,2048]{1,0:T(8,128)(2,1)S(1)}, u32[]{:S(2)}, u32[]{:S(2)}) collective-permute-start(bf16[32,2048]{1,0:T(8,128)(2,1)S(1)} %get-tuple-element.103), channel_id=1, source_target_pairs={{0,2},{1,3},{2,0},{3,1},{4,6},{5,7},{6,4},{7,5},{8,10},{9,11},{10,... | collective-permute-start | bytes 393224 | tf_op jit(solution)/shard_map/ppermute | solution.py:416
  91.1 12.8 %collective-permute-start.22 = (bf16[32,2048]{1,0:T(8,128)(2,1)S(1)}, bf16[32,2048]{1,0:T(8,128)(2,1)S(1)}, u32[]{:S(2)}, u32[]{:S(2)}) collective-permute-start(bf16[32,2048]{1,0:T(8,128)(2,1)S(1)} %get-tuple-element.104), channel_id=1, source_target_pairs={{0,3},{1,2},{2,1},{3,0},{4,7},{5,6},{6,5},{7,4},{8,11},{9,10},{10,... | collective-permute-start | bytes 393224 | tf_op jit(solution)/shard_map/ppermute | solution.py:416
  94.0 10.1 %collective-permute-start.12 = (bf16[32,2048]{1,0:T(8,128)(2,1)S(1)}, bf16[32,2048]{1,0:T(8,128)(2,1)S(1)}, u32[]{:S(2)}, u32[]{:S(2)}) collective-permute-start(bf16[32,2048]{1,0:T(8,128)(2,1)S(1)} %get-tuple-element.92), channel_id=1, source_target_pairs={{0,1},{1,0},{2,3},{3,2},{4,5},{5,4},{6,7},{7,6},{8,9},{9,8},{10,11... | collective-permute-start | bytes 393224 | tf_op jit(solution)/shard_map/ppermute | solution.py:416
  95.9 9.7 %collective-permute-start.13 = (bf16[32,2048]{1,0:T(8,128)(2,1)S(1)}, bf16[32,2048]{1,0:T(8,128)(2,1)S(1)}, u32[]{:S(2)}, u32[]{:S(2)}) collective-permute-start(bf16[32,2048]{1,0:T(8,128)(2,1)S(1)} %get-tuple-element.93), channel_id=1, source_target_pairs={{0,2},{1,3},{2,0},{3,1},{4,6},{5,7},{6,4},{7,5},{8,10},{9,11},{10,... | collective-permute-start | bytes 393224 | tf_op jit(solution)/shard_map/ppermute | solution.py:416
  99.1 20.0 %collective-permute-start.3 = (bf16[128,768]{1,0:T(8,128)(2,1)S(1)}, bf16[128,768]{1,0:T(8,128)(2,1)S(1)}, u32[]{:S(2)}, u32[]{:S(2)}) collective-permute-start(bf16[128,768]{1,0:T(8,128)(2,1)S(1)} %shard_map.69), channel_id=1, source_target_pairs={{0,28},{4,24},{8,20},{12,16},{16,12},{20,8},{24,4},{28,0},{1,29},{... | collective-permute-start | bytes 589832 | tf_op jit(solution)/shard_map/ppermute | solution.py:414
  103.4 5.4 %collective-permute-start.14 = (bf16[32,2048]{1,0:T(8,128)(2,1)S(1)}, bf16[32,2048]{1,0:T(8,128)(2,1)S(1)}, u32[]{:S(2)}, u32[]{:S(2)}) collective-permute-start(bf16[32,2048]{1,0:T(8,128)(2,1)S(1)} %get-tuple-element.94), channel_id=1, source_target_pairs={{0,3},{1,2},{2,1},{3,0},{4,7},{5,6},{6,5},{7,4},{8,11},{9,10},{10,... | collective-permute-start | bytes 393224 | tf_op jit(solution)/shard_map/ppermute | solution.py:416
  103.9 5.6 %collective-permute-start.16 = (bf16[32,2048]{1,0:T(8,128)(2,1)S(1)}, bf16[32,2048]{1,0:T(8,128)(2,1)S(1)}, u32[]{:S(2)}, u32[]{:S(2)}) collective-permute-start(bf16[32,2048]{1,0:T(8,128)(2,1)S(1)} %get-tuple-element.97), channel_id=1, source_target_pairs={{0,1},{1,0},{2,3},{3,2},{4,5},{5,4},{6,7},{7,6},{8,9},{9,8},{10,11... | collective-permute-start | bytes 393224 | tf_op jit(solution)/shard_map/ppermute | solution.py:416
  104.2 8.3 %collective-permute-start.17 = (bf16[32,2048]{1,0:T(8,128)(2,1)S(1)}, bf16[32,2048]{1,0:T(8,128)(2,1)S(1)}, u32[]{:S(2)}, u32[]{:S(2)}) collective-permute-start(bf16[32,2048]{1,0:T(8,128)(2,1)S(1)} %get-tuple-element.98), channel_id=1, source_target_pairs={{0,2},{1,3},{2,0},{3,1},{4,6},{5,7},{6,4},{7,5},{8,10},{9,11},{10,... | collective-permute-start | bytes 393224 | tf_op jit(solution)/shard_map/ppermute | solution.py:416
  105.6 8.9 %collective-permute-start.18 = (bf16[32,2048]{1,0:T(8,128)(2,1)S(1)}, bf16[32,2048]{1,0:T(8,128)(2,1)S(1)}, u32[]{:S(2)}, u32[]{:S(2)}) collective-permute-start(bf16[32,2048]{1,0:T(8,128)(2,1)S(1)} %get-tuple-element.99), channel_id=1, source_target_pairs={{0,3},{1,2},{2,1},{3,0},{4,7},{5,6},{6,5},{7,4},{8,11},{9,10},{10,... | collective-permute-start | bytes 393224 | tf_op jit(solution)/shard_map/ppermute | solution.py:416
  108.8 7.8 %collective-permute-start.32 = (bf16[32,1280]{1,0:T(8,128)(2,1)S(1)}, bf16[32,1280]{1,0:T(8,128)(2,1)S(1)}, u32[]{:S(2)}, u32[]{:S(2)}) collective-permute-start(bf16[32,1280]{1,0:T(8,128)(2,1)S(1)} %get-tuple-element.133), channel_id=1, source_target_pairs={{0,1},{1,0},{2,3},{3,2},{4,5},{5,4},{6,7},{7,6},{8,9},{9,8},{10,11... | collective-permute-start | bytes 245768 | tf_op jit(solution)/shard_map/ppermute | solution.py:416
  109.5 7.5 %collective-permute-start.33 = (bf16[32,1280]{1,0:T(8,128)(2,1)S(1)}, bf16[32,1280]{1,0:T(8,128)(2,1)S(1)}, u32[]{:S(2)}, u32[]{:S(2)}) collective-permute-start(bf16[32,1280]{1,0:T(8,128)(2,1)S(1)} %get-tuple-element.134), channel_id=1, source_target_pairs={{0,2},{1,3},{2,0},{3,1},{4,6},{5,7},{6,4},{7,5},{8,10},{9,11},{10,... | collective-permute-start | bytes 245768 | tf_op jit(solution)/shard_map/ppermute | solution.py:416
  112.5 5.5 %collective-permute-start.34 = (bf16[32,1280]{1,0:T(8,128)(2,1)S(1)}, bf16[32,1280]{1,0:T(8,128)(2,1)S(1)}, u32[]{:S(2)}, u32[]{:S(2)}) collective-permute-start(bf16[32,1280]{1,0:T(8,128)(2,1)S(1)} %get-tuple-element.135), channel_id=1, source_target_pairs={{0,3},{1,2},{2,1},{3,0},{4,7},{5,6},{6,5},{7,4},{8,11},{9,10},{10,... | collective-permute-start | bytes 245768 | tf_op jit(solution)/shard_map/ppermute | solution.py:416
  119.1 11.9 %copy-start.3 = (s32[8,512]{1,0:T(8,128)S(1)}, s32[8,512]{1,0:T(8,128)}, u32[]{:S(2)}) copy-start(s32[8,512]{1,0:T(8,128)} %get-tuple-element.72.key_hbm.key_ref) | copy-start | bytes 49156
